TPU v7x, 32 devices: a whole 2x2x4 slice. The times are simulated.
32 devices in a mesh: dp: 8 (over z, x), chan: 4 (over y, core).
Axes of the slice: x: 2, y: 2, z: 4, core: 2. Of those that a mesh axis runs over, the one named last changes fastest.
Arguments:
- inputs: bfloat16 [32768, 512], P('dp', 'chan'), may hold values from -6 to 6
- condition: float32 [2048, 1152], P('dp'), may hold values from -36 to 36
- lengths: int32 [2048], P('dp'), may hold values from 4 to 16
- cotangent: bfloat16 [16384, 512], P('dp', 'chan'), may hold values from -6 to 6
- conv1_w: float32 [512, 5, 512], P('dp', None, 'chan'), may hold values from -0.125 to 0.125
- conv1_m: float32 [512, 5, 512], P('dp', None, 'chan'), as said below
- conv1_v: float32 [512, 5, 512], P('dp', None, 'chan'), as said below
- conv2_w: float32 [512, 5, 512], P('dp', None, 'chan'), may hold values from -0.125 to 0.125
- conv2_m: float32 [512, 5, 512], P('dp', None, 'chan'), as said below
- conv2_v: float32 [512, 5, 512], P('dp', None, 'chan'), as said below
- res_w: float32 [512, 512], P('dp', 'chan'), may hold values from -0.25 to 0.25
- res_m: float32 [512, 512], P('dp', 'chan'), as said below
- res_v: float32 [512, 512], P('dp', 'chan'), as said below
- down_w: float32 [512, 3, 512], P('dp', None, 'chan'), may hold values from -0.15625 to 0.15625
- down_m: float32 [512, 3, 512], P('dp', None, 'chan'), as said below
- down_v: float32 [512, 3, 512], P('dp', None, 'chan'), as said below
- film_w: float32 [1152, 2, 512], P('dp', None, 'chan'), may hold values from -0.1875 to 0.1875
- film_m: float32 [1152, 2, 512], P('dp', None, 'chan'), as said below
- film_v: float32 [1152, 2, 512], P('dp', None, 'chan'), as said below
- small_w: float32 [10, 512], P(None, 'chan'), may hold values from -1 to 2, as said below
- small_m: float32 [10, 512], P(None, 'chan'), as said below
- small_v: float32 [10, 512], P(None, 'chan'), as said below
Outputs:
- output: bfloat16 [16384, 512], P('dp', 'chan')
- input_grad: bfloat16 [32768, 512], P('dp', 'chan')
- conv1_m_new: float32 [512, 5, 512], P('dp', None, 'chan')
- conv1_v_new: float32 [512, 5, 512], P('dp', None, 'chan')
- conv1_w_new: float32 [512, 5, 512], P('dp', None, 'chan')
- conv2_m_new: float32 [512, 5, 512], P('dp', None, 'chan')
- conv2_v_new: float32 [512, 5, 512], P('dp', None, 'chan')
- conv2_w_new: float32 [512, 5, 512], P('dp', None, 'chan')
- res_m_new: float32 [512, 512], P('dp', 'chan')
- res_v_new: float32 [512, 512], P('dp', 'chan')
- res_w_new: float32 [512, 512], P('dp', 'chan')
- down_m_new: float32 [512, 3, 512], P('dp', None, 'chan')
- down_v_new: float32 [512, 3, 512], P('dp', None, 'chan')
- down_w_new: float32 [512, 3, 512], P('dp', None, 'chan')
- film_m_new: float32 [1152, 2, 512], P('dp', None, 'chan')
- film_v_new: float32 [1152, 2, 512], P('dp', None, 'chan')
- film_w_new: float32 [1152, 2, 512], P('dp', None, 'chan')
- small_m_new: float32 [10, 512], P(None, 'chan')
- small_v_new: float32 [10, 512], P(None, 'chan')
- small_w_new: float32 [10, 512], P(None, 'chan')
Inputs may be any that keep to these rules, and one draw needn't show every extreme that they name: `lengths`: frames from a sample's length on are padding. `conv1_m`: old first moments. `conv1_v`: old second moments, positive. `conv2_m`: old first moments. `conv2_v`: old second moments, positive. `res_m`: old first moments. `res_v`: old second moments, positive. `down_m`: old first moments. `down_v`: old second moments, positive. `film_m`: old first moments. `film_v`: old second moments, positive. `small_w`: biases and norm parameters. `small_m`: old first moments. `small_v`: old second moments, positive.
All inputs are finite; a program needn't handle non-finite values.
Results may differ from a plain program's by a relative error of at most 0.017.
Values may be sent and summed in bfloat16 or wider, within the bound.
A program may use at most 192 MiB of HBM per device.

v0:
```python
from functools import partial

import jax
import jax.numpy as jnp
from jax import lax
from jax.sharding import PartitionSpec as P

C = 512
GROUPS = 8


eps_norm = 1e-05
beta_one = 0.9
beta_two = 0.999
adam_eps = 1e-08
weight_decay = 0.01
rate_large = 0.05
rate_small = 0.3
adam_step = 10


def split_up(array, dim, peers):
    before, after = (array.shape[:dim], array.shape[dim + 1 :])
    return jnp.moveaxis(array.reshape(*before, peers, -1, *after), dim, 0)


def summed_on_arrival(array, axis, dim):
    peers = lax.axis_size(axis)
    parts = lax.all_to_all(split_up(array, dim, peers), axis, 0, 0, tiled=True)
    return jnp.sum(parts.astype(jnp.float32), axis=0)


def sent_together(arrays, axis, dim, along):
    columns = [a.reshape(*a.shape[:along], -1) for a in arrays]
    both = jnp.concatenate(columns, axis=along)
    result, at, done = (summed_on_arrival(both, axis, dim), 0, [])
    for a, column in zip(arrays, columns):
        slab = result[..., at : at + column.shape[along]]
        done.append(slab.reshape(*slab.shape[:along], *a.shape[along:]))
        at += column.shape[along]
    return tuple(done)


def mish(values):
    return values * jnp.tanh(jax.nn.softplus(values))


def group_norm(pre_norm, valid_mask, gain_row, shift_row):
    samples, frames, channels = pre_norm.shape
    group_size = C // GROUPS
    grouped = pre_norm.reshape(samples, frames, channels // group_size, group_size)
    weights_in = valid_mask[:, :, None, None]
    counted = (jnp.sum(valid_mask, axis=1) * group_size).reshape(samples, 1, 1, 1)
    centre = jnp.sum(grouped * weights_in, axis=(1, 3), keepdims=True) / counted
    shifted = grouped - centre
    spread_sq = jnp.sum(jnp.square(shifted * weights_in), axis=(1, 3), keepdims=True) / counted
    normed = (shifted * lax.rsqrt(spread_sq + eps_norm)).reshape(samples, frames, channels)
    return normed * gain_row + shift_row


def first_section(valid_mask, conv_out, bias_row, gain_row, shift_row, film_scale, film_shift):
    normed = group_norm(conv_out + bias_row, valid_mask, gain_row, shift_row)
    return (film_scale[:, None, :] * mish(normed) + film_shift[:, None, :]) * valid_mask[:, :, None]


def second_section(valid_mask, conv_out, res_out, bias_row, gain_row, shift_row, res_bias):
    normed = group_norm(conv_out + bias_row, valid_mask, gain_row, shift_row)
    return (mish(normed) + res_out + res_bias) * valid_mask[:, :, None]


def taps_sum(products, samples, kernel, local_width):
    frames = products.shape[0] // samples
    half_k = kernel // 2
    padded_grid = jnp.pad(
        products.reshape(samples, frames, kernel, local_width),
        ((0, 0), (half_k, half_k), (0, 0), (0, 0)),
    )
    summed = padded_grid[:, 0:frames, 0, :]
    for offset in range(1, kernel):
        summed = summed + padded_grid[:, offset : offset + frames, offset, :]
    return summed


def taps_spread(gradient, kernel):
    samples, frames, local_width = gradient.shape
    half_k = kernel // 2
    padded = jnp.pad(gradient, ((0, 0), (half_k, half_k), (0, 0)))
    pieces_list = [
        padded[:, 2 * half_k - offset : 2 * half_k - offset + frames, :] for offset in range(kernel)
    ]
    return jnp.stack(pieces_list, axis=2).reshape(samples * frames, kernel * local_width)


def stride_sum(products, samples, local_width):
    frames = products.shape[0] // samples
    padded_grid = jnp.pad(
        products.reshape(samples, frames, 3, local_width), ((0, 0), (1, 1), (0, 0), (0, 0))
    )
    return (
        padded_grid[:, 0:frames:2, 0, :]
        + padded_grid[:, 1 : frames + 1 : 2, 1, :]
        + padded_grid[:, 2 : frames + 2 : 2, 2, :]
    )


def stride_spread(gradient):
    samples, halves, local_width = gradient.shape
    blank = jnp.zeros_like(gradient)
    later = jnp.concatenate([gradient[:, 1:], blank[:, :1]], axis=1)
    even_rows = jnp.stack([blank, gradient, blank], axis=2)
    odd_rows = jnp.stack([later, blank, gradient], axis=2)
    return jnp.stack([even_rows, odd_rows], axis=2).reshape(samples * halves * 2, 3 * local_width)


def contract(local_rows, matrix):
    gathered = lax.all_gather(local_rows, "chan", axis=1, tiled=True)
    return (jnp.dot(gathered, matrix, preferred_element_type=jnp.float32), gathered)


def outer(kept_rows, gradient):
    return lax.dot_general(
        kept_rows, gradient, (((0,), (0,)), ((), ())), preferred_element_type=jnp.float32
    )


def reduce_channels(partial_sum):
    return lax.psum_scatter(
        partial_sum.astype(jnp.bfloat16), "chan", scatter_dimension=1, tiled=True
    ).astype(jnp.float32)


def transposed(gradient, matrix):
    return lax.dot_general(
        gradient, matrix, (((1,), (1,)), ((), ())), preferred_element_type=jnp.float32
    )


def adam_update(weight, gradient, old_first, old_second, learn_rate, decay_term):
    first_new = beta_one * old_first + (1.0 - beta_one) * gradient
    second_new = beta_two * old_second + (1.0 - beta_two) * gradient * gradient
    step_size = (
        first_new
        / (1.0 - beta_one**adam_step)
        / (jnp.sqrt(second_new / (1.0 - beta_two**adam_step)) + adam_eps)
    )
    return (first_new, second_new, weight - learn_rate * (step_size + decay_term * weight))


def body(
    inputs,
    condition,
    lengths,
    cotangent,
    conv1_w,
    conv1_m,
    conv1_v,
    conv2_w,
    conv2_m,
    conv2_v,
    res_w,
    res_m,
    res_v,
    down_w,
    down_m,
    down_v,
    film_w,
    film_m,
    film_v,
    small_w,
    small_m,
    small_v,
):
    low_type = jnp.bfloat16
    samples = lengths.shape[0]
    frames = inputs.shape[0] // samples
    valid_mask = (jnp.arange(frames)[None, :] < lengths[:, None]).astype(jnp.float32)
    half_mask = (2 * jnp.arange(frames // 2)[None, :] < lengths[:, None]).astype(jnp.float32)
    col_high, col_negative = lax.pmax(
        (jnp.max(condition, axis=0), -jnp.min(condition, axis=0)), "dp"
    )
    col_low = -col_negative
    normed_cond = 2.0 * (condition - col_low) / jnp.maximum(col_high - col_low, 1.0) - 1.0
    cond_act = mish(normed_cond).astype(low_type)
    full_one, full_two, full_res, full_down, full_film = (
        lax.all_gather(conv1_w.astype(low_type), "dp", axis=0, tiled=True),
        lax.all_gather(conv2_w.astype(low_type), "dp", axis=0, tiled=True),
        lax.all_gather(res_w.astype(low_type), "dp", axis=0, tiled=True),
        lax.all_gather(down_w.astype(low_type), "dp", axis=0, tiled=True),
        lax.all_gather(film_w.astype(low_type), "dp", axis=0, tiled=True),
    )
    in_chans, kernel, local_width = full_one.shape
    cond_width = full_film.shape[0]
    film_out = jnp.dot(
        cond_act, full_film.reshape(cond_width, 2 * local_width), preferred_element_type=jnp.float32
    )
    film_scale = film_out[:, :local_width] + small_w[6]
    film_shift = film_out[:, local_width:] + small_w[7]
    frame_mask = valid_mask.reshape(samples * frames, 1)
    masked_in = inputs * frame_mask.astype(low_type)
    joint_fwd = jnp.concatenate(
        [full_one.reshape(in_chans, kernel * local_width), full_res], axis=1
    )
    prod_one, kept_in = contract(masked_in, joint_fwd)
    conv_one = taps_sum(prod_one[:, : kernel * local_width], samples, kernel, local_width)
    res_out = prod_one[:, kernel * local_width :].reshape(samples, frames, local_width)
    section_one, back_one = jax.vjp(
        partial(first_section, valid_mask),
        conv_one,
        small_w[0],
        small_w[1],
        small_w[2],
        film_scale,
        film_shift,
    )
    hidden = section_one.astype(low_type).reshape(samples * frames, local_width)
    prod_two, kept_hidden = contract(hidden, full_two.reshape(in_chans, kernel * local_width))
    conv_two = taps_sum(prod_two, samples, kernel, local_width)
    section_two, back_two = jax.vjp(
        partial(second_section, valid_mask),
        conv_two,
        res_out,
        small_w[3],
        small_w[4],
        small_w[5],
        small_w[8],
    )
    block_out = section_two.astype(low_type).reshape(samples * frames, local_width)
    prod_down, kept_out = contract(block_out, full_down.reshape(in_chans, 3 * local_width))
    result = (stride_sum(prod_down, samples, local_width) + small_w[9]) * half_mask[:, :, None]
    output = result.astype(low_type).reshape(samples * (frames // 2), local_width)
    grad_out = cotangent.reshape(samples, frames // 2, local_width) * half_mask[:, :, None].astype(
        low_type
    )
    down_grads = stride_spread(grad_out)
    back_one_w, back_two_w, back_res_w, back_down_w = (
        lax.all_gather(conv1_w.astype(low_type), "dp", axis=0, tiled=True),
        lax.all_gather(conv2_w.astype(low_type), "dp", axis=0, tiled=True),
        lax.all_gather(res_w.astype(low_type), "dp", axis=0, tiled=True),
        lax.all_gather(down_w.astype(low_type), "dp", axis=0, tiled=True),
    )
    grad_down = outer(kept_out, down_grads)
    part_out = transposed(down_grads, back_down_w.reshape(in_chans, 3 * local_width))
    grad_block = reduce_channels(part_out).reshape(samples, frames, local_width)
    grad_conv_two, grad_res, grad_bias_two, grad_gain_two, grad_shift_two, grad_res_bias = back_two(
        grad_block
    )
    taps_two = taps_spread(grad_conv_two.astype(low_type), kernel)
    grad_two = outer(kept_hidden, taps_two)
    part_hidden = transposed(taps_two, back_two_w.reshape(in_chans, kernel * local_width))
    grad_hidden = reduce_channels(part_hidden).reshape(samples, frames, local_width)
    grad_conv_one, grad_bias_one, grad_gain_one, grad_shift_one, grad_scale, grad_offset = back_one(
        grad_hidden
    )
    film_grads = jnp.concatenate([grad_scale, grad_offset], axis=1).astype(low_type)
    grad_film = lax.dot_general(
        cond_act, film_grads, (((0,), (0,)), ((), ())), preferred_element_type=jnp.float32
    ).reshape(cond_width, 2, local_width)
    taps_one = jnp.concatenate(
        [
            taps_spread(grad_conv_one.astype(low_type), kernel),
            grad_res.astype(low_type).reshape(samples * frames, local_width),
        ],
        axis=1,
    )
    grad_joint = outer(kept_in, taps_one)
    joint_back = jnp.concatenate(
        [back_one_w.reshape(in_chans, kernel * local_width), back_res_w], axis=1
    )
    part_input = transposed(taps_one, joint_back)
    grad_input = reduce_channels(part_input)
    input_grad = (grad_input * frame_mask).astype(low_type)
    small_grad = jnp.stack(
        [
            grad_bias_one,
            grad_gain_one,
            grad_shift_one,
            grad_bias_two,
            grad_gain_two,
            grad_shift_two,
            jnp.sum(grad_scale, axis=0),
            jnp.sum(grad_offset, axis=0),
            grad_res_bias,
            jnp.sum(grad_out.astype(jnp.float32), axis=(0, 1)),
        ]
    )
    small_total = lax.psum(small_grad, "dp")
    sum_one, sum_two, sum_res, sum_down, sum_film = (
        *sent_together(
            (
                grad_joint[:, : kernel * local_width]
                .reshape(in_chans, kernel, local_width)
                .astype(jnp.bfloat16),
                grad_two.reshape(in_chans, kernel, local_width).astype(jnp.bfloat16),
                grad_joint[:, kernel * local_width :].astype(jnp.bfloat16),
                grad_down.reshape(in_chans, 3, local_width).astype(jnp.bfloat16),
            ),
            "dp",
            0,
            1,
        ),
        summed_on_arrival(grad_film.astype(jnp.bfloat16), "dp", 0),
    )
    one_m, one_v, one_w = adam_update(conv1_w, sum_one, conv1_m, conv1_v, rate_large, weight_decay)
    two_m, two_v, two_w = adam_update(conv2_w, sum_two, conv2_m, conv2_v, rate_large, weight_decay)
    res_m2, res_v2, res_w2 = adam_update(res_w, sum_res, res_m, res_v, rate_large, weight_decay)
    down_m2, down_v2, down_w2 = adam_update(
        down_w, sum_down, down_m, down_v, rate_large, weight_decay
    )
    film_m2, film_v2, film_w2 = adam_update(
        film_w, sum_film, film_m, film_v, rate_large, weight_decay
    )
    small_m2, small_v2, small_w2 = adam_update(
        small_w, small_total, small_m, small_v, rate_small, 0.0
    )
    return (
        output,
        input_grad,
        one_m,
        one_v,
        one_w,
        two_m,
        two_v,
        two_w,
        res_m2,
        res_v2,
        res_w2,
        down_m2,
        down_v2,
        down_w2,
        film_m2,
        film_v2,
        film_w2,
        small_m2,
        small_v2,
        small_w2,
    )


def solution(mesh):
    in_specs = (
        P("dp", "chan"),
        P("dp", None),
        P("dp"),
        P("dp", "chan"),
        P("dp", None, "chan"),
        P("dp", None, "chan"),
        P("dp", None, "chan"),
        P("dp", None, "chan"),
        P("dp", None, "chan"),
        P("dp", None, "chan"),
        P("dp", "chan"),
        P("dp", "chan"),
        P("dp", "chan"),
        P("dp", None, "chan"),
        P("dp", None, "chan"),
        P("dp", None, "chan"),
        P("dp", None, "chan"),
        P("dp", None, "chan"),
        P("dp", None, "chan"),
        P(None, "chan"),
        P(None, "chan"),
        P(None, "chan"),
    )
    out_specs = (
        P("dp", "chan"),
        P("dp", "chan"),
        P("dp", None, "chan"),
        P("dp", None, "chan"),
        P("dp", None, "chan"),
        P("dp", None, "chan"),
        P("dp", None, "chan"),
        P("dp", None, "chan"),
        P("dp", "chan"),
        P("dp", "chan"),
        P("dp", "chan"),
        P("dp", None, "chan"),
        P("dp", None, "chan"),
        P("dp", None, "chan"),
        P("dp", None, "chan"),
        P("dp", None, "chan"),
        P("dp", None, "chan"),
        P(None, "chan"),
        P(None, "chan"),
        P(None, "chan"),
    )
    return jax.shard_map(body, mesh=mesh, in_specs=in_specs, out_specs=out_specs, check_vma=False)
```

profile of v0, /device:TPU:8, one launch (start us, length us, event | category | flops | bytes accessed | tf_op | source)
XLA Modules:
  0.0 595.0 jit_solution(2664562738864604932)
XLA Ops:
  12.0 28.6 %all_gather.35 = bf16[512,3,128]{2,0,1:T(8,128)(2,1)S(1)} all-gather(bf16[64,3,128]{2,0,1:T(8,128)(2,1)S(1)} %convert_element_type.167), channel_id=1, replica_groups=mesh['dp'=8,'chan'=4] {'dp'}, dimensions={0}, use_global_device_ids=true | all-gather | bytes 442368 | tf_op jit(solution)/shard_map/all_gather | solution.py:188
  53.1 6.4 %copy.295 = bf16[4096,512]{0,1:T(8,128)(2,1)} copy(bf16[4096,512]{1,0:T(8,128)(2,1)} %convolution_convert_fusion.1) | data formatting | bytes 8388608
  60.9 30.5 %all_gather.31 = bf16[512,128]{1,0:T(8,128)(2,1)S(1)} all-gather(bf16[64,128]{1,0:T(8,128)(2,1)S(1)} %convert_element_type.162), channel_id=1, replica_groups=mesh['dp'=8,'chan'=4] {'dp'}, dimensions={0}, use_global_device_ids=true | all-gather | bytes 147456 | tf_op jit(solution)/shard_map/all_gather | solution.py:187
  91.6 31.4 %all_gather.30 = bf16[512,5,128]{2,0,1:T(8,128)(2,1)S(1)} all-gather(bf16[64,5,128]{2,0,1:T(8,128)(2,1)S(1)} %convert_element_type.161), channel_id=1, replica_groups=mesh['dp'=8,'chan'=4] {'dp'}, dimensions={0}, use_global_device_ids=true | all-gather | bytes 737280 | tf_op jit(solution)/shard_map/all_gather | solution.py:185
  123.3 37.5 %all-reduce.6 = (f32[1152]{0:T(1024)S(1)}, f32[1152]{0:T(1024)S(1)}) all-reduce(f32[1152]{0:T(1024)S(1)} %get-tuple-element.100, f32[1152]{0:T(1024)S(1)} %neg.19), channel_id=1, replica_groups=mesh['dp'=8,'chan'=4] {'dp'}, use_global_device_ids=true, to_apply=%region_3.0 | all-reduce | flops 2304 | bytes 18432 | tf_op jit(solution)/shard_map/pmax | solution.py:178
  161.5 31.5 %all_gather.28 = bf16[1152,2,128]{2,1,0:T(2,128)(2,1)S(1)} all-gather(bf16[144,2,128]{2,1,0:T(2,128)(2,1)S(1)} %convert_element_type.157), channel_id=1, replica_groups=mesh['dp'=8,'chan'=4] {'dp'}, dimensions={0}, use_global_device_ids=true | all-gather | bytes 663552 | tf_op jit(solution)/shard_map/all_gather | solution.py:189
  209.4 13.8 %reshape.613 = f32[256,16,5,128]{3,2,1,0:T(8,128)} reshape(f32[4096,640]{1,0:T(8,128)} %slice.176) | data formatting | bytes 20971520 | tf_op jit(solution)/shard_map/reshape | solution.py:75
  223.3 15.7 %copy.237 = f32[256,16,5,128]{3,0,2,1:T(8,128)} copy(f32[256,16,5,128]{3,2,1,0:T(8,128)} %reshape.613) | data formatting | bytes 20971520 | tf_op jit(solution)/shard_map/reshape | solution.py:75
  250.5 31.5 %all_gather.33 = bf16[512,5,128]{2,0,1:T(8,128)(2,1)S(1)} all-gather(bf16[64,5,128]{2,0,1:T(8,128)(2,1)S(1)} %convert_element_type.165), channel_id=1, replica_groups=mesh['dp'=8,'chan'=4] {'dp'}, dimensions={0}, use_global_device_ids=true | all-gather | bytes 737280 | tf_op jit(solution)/shard_map/all_gather | solution.py:186
  289.3 6.4 %copy.248 = bf16[4096,512]{1,0:T(8,128)(2,1)} copy(bf16[4096,512]{0,1:T(8,128)(2,1)} %all-gather.6.cloned.1.call-done) | data formatting | bytes 8388608 | tf_op jit(solution)/shard_map/all_gather | solution.py:116
  295.7 10.3 %fusion.7 = f32[256,16,5,128]{3,0,2,1:T(8,128)S(1)} fusion(bf16[256,16,512,1]{2,1,0,3:T(8,128)(2,1)} %bitcast.268, bf16[512,5,128]{0,2,1:T(8,128)(2,1)} %copy.249), kind=kOutput, calls=%fused_computation.27 | convolution fusion | flops 2684354560 | bytes 15335424 | tf_op jit(solution)/shard_map/dot_general | solution.py:117
  321.0 7.6 %multiply_reduce_fusion.1 = (f32[128]{0:T(128)}, f32[256,128]{1,0:T(8,128)}, f32[128]{0:T(128)}, f32[256,16,128]{2,0,1:T(8,128)}, bf16[256,16,128]{2,0,1:T(8,128)(2,1)}) fusion(f32[256,16,1,128]{3,0,2,1:T(8,128)} %get-tuple-element.133, f32[256,128]{1,0:T(8,128)} %copy.255, f32[256,128]{1,0:T(8,128)S(1)} %copy.252, f32[128]{0:T(128)} %get-tuple-element.150, ...), kind=kLoop, calls=%fused_computation.67 | loop fusion | flops 18841344 | bytes 9849856 | tf_op jit(solution)/shard_map/transpose(jvp())/reduce_sum | solution.py:58
  350.1 6.3 %copy.269 = bf16[256,16,5,128]{3,2,1,0:T(8,128)(2,1)S(1)} copy(bf16[256,16,5,128]{3,0,1,2:T(8,128)(2,1)} %fusion.61) | data formatting | bytes 10485760 | tf_op jit(solution)/shard_map/stack | solution.py:91
  364.6 6.4 %copy.297 = bf16[4096,512]{0,1:T(8,128)(2,1)} copy(bf16[4096,512]{1,0:T(8,128)(2,1)} %convolution_convert_fusion.2) | data formatting | bytes 8388608
  376.3 39.2 %reduce-scatter.12.cloned.1.call-done = bf16[128,4096]{1,0:T(8,128)(2,1)} async-done(((bf16[512,4096]{1,0:T(8,128)(2,1)}), bf16[128,4096]{1,0:T(8,128)(2,1)}) %reduce-scatter.12.cloned.1.call-update) | async-done | bytes 1048592
  442.2 6.3 %copy.275 = bf16[256,16,5,128]{3,2,1,0:T(8,128)(2,1)S(1)} copy(bf16[256,16,5,128]{3,0,1,2:T(8,128)(2,1)} %fusion.69) | data formatting | bytes 10485760 | tf_op jit(solution)/shard_map/stack | solution.py:91
  457.6 6.4 %copy.299 = bf16[4096,512]{0,1:T(8,128)(2,1)} copy(bf16[4096,512]{1,0:T(8,128)(2,1)} %convolution_convert_fusion) | data formatting | bytes 8388608
  470.0 8.0 %copy.364 = bf16[512,8,5,128]{3,1,2,0:T(8,128)(2,1)} copy(bf16[512,8,5,128]{3,2,1,0:T(8,128)(2,1)} %bitcast.265) | data formatting | bytes 10485760
  478.1 8.1 %copy.276 = bf16[640,4096]{1,0:T(8,128)(2,1)} copy(bf16[640,4096]{0,1:T(8,128)(2,1)} %bitcast.269) | data formatting | bytes 10485760 | tf_op jit(solution)/shard_map/dot_general | solution.py:121
  486.1 6.8 %fusion.45 = bf16[512,5,128]{2,0,1:T(8,128)(2,1)S(1)} fusion(bf16[5,128,4096]{2,1,0:T(8,128)(2,1)} %bitcast.279, bf16[4096,512]{0,1:T(8,128)(2,1)} %all-gather.6.cloned.1.call-done), kind=kOutput, calls=%fused_computation.97 | convolution fusion | flops 2684682240 | bytes 10092544 | tf_op jit(solution)/shard_map/dot_general | solution.py:121
  501.9 6.0 %all-to-all-start.1 = ((bf16[8,144,2,128]{3,2,1,0:T(2,128)(2,1)}), bf16[8,144,2,128]{3,2,1,0:T(2,128)(2,1)S(1)}, u32[]{:S(2)}, u32[]{:S(2)}) async-start(bf16[8,144,2,128]{3,2,1,0:T(2,128)(2,1)} %convert_element_type.186), calls=%async_computation.1 | async-start | bytes 1179648 | tf_op jit(solution)/shard_map/all_to_all | solution.py:29
  507.9 7.6 %fusion.44 = bf16[512,768]{1,0:T(8,128)(2,1)S(1)} fusion(bf16[4096,512]{1,0:T(8,128)(2,1)} %all-gather.4.cloned.1.call-done, bf16[4096,128]{1,0:T(8,128)(2,1)} %copy-done.17, bf16[4096,640]{1,0:T(8,128)(2,1)} %bitcast.278), kind=kOutput, calls=%fused_computation.96 | convolution fusion | flops 3234201600 | bytes 11272192 | tf_op jit(solution)/shard_map/dot_general | solution.py:121
  528.2 6.5 %copy.259 = bf16[4096,512]{1,0:T(8,128)(2,1)} copy(bf16[4096,512]{0,1:T(8,128)(2,1)} %all-gather.8.cloned.1.call-done) | data formatting | bytes 8388608 | tf_op jit(solution)/shard_map/all_gather | solution.py:116
  542.1 36.2 %psum.7 = f32[10,128]{1,0:T(8,128)S(1)} all-reduce(f32[10,128]{1,0:T(8,128)S(1)} %stack.117), channel_id=1, replica_groups=mesh['dp'=8,'chan'=4] {'dp'}, use_global_device_ids=true, to_apply=%region_38.40 | all-reduce | flops 1280 | bytes 10240 | tf_op jit(solution)/shard_map/psum | solution.py:286
  (299 shorter events, 184.0 us)
Async XLA Ops:
  7.2 187.2 %all-gather.4.cloned.1.call-start = ((), (), s32[]{:S(2)}) async-start(), calls=%async_computation.5 | async-start | bytes 5242880 | tf_op jit(solution)/shard_map/all_gather | solution.py:116
  11.4 274.8 %reduce-scatter.10.cloned.1.call-start = ((), (), s32[]{:S(2)}) async-start(), calls=%async_computation.8 | async-start | bytes 5242880
  59.5 229.8 %all-gather.6.cloned.1.call-start = ((), (), s32[]{:S(2)}) async-start(), calls=%async_computation.6 | async-start | bytes 5242880 | tf_op jit(solution)/shard_map/all_gather | solution.py:116
  60.2 100.8 %copy-start.45 = (f32[10,128]{1,0:T(8,128)S(1)}, f32[10,128]{1,0:T(8,128)}, u32[]{:S(2)}) copy-start(f32[10,128]{1,0:T(8,128)} %param.42) | copy-start | bytes 15364
  91.6 103.3 %copy-start.39 = (bf16[512,128]{0,1:T(8,128)(2,1)}, bf16[512,128]{0,1:T(8,128)(2,1)S(1)}, u32[]{:S(2)}) copy-start(bf16[512,128]{0,1:T(8,128)(2,1)S(1)} %copy.236) | copy-start | bytes 393220
  123.3 71.6 %copy-start.21 = (bf16[512,5,128]{0,2,1:T(8,128)(2,1)}, bf16[512,5,128]{0,2,1:T(8,128)(2,1)S(1)}, u32[]{:S(2)}) copy-start(bf16[512,5,128]{0,2,1:T(8,128)(2,1)S(1)} %copy.235) | copy-start | bytes 1966084
  161.0 83.5 %copy-start.43 = (f32[256]{0:T(256)}, f32[256]{0:T(256)S(1)}, u32[]{:S(2)}) copy-start(f32[256]{0:T(256)S(1)} %broadcast_multiply_fusion.1) | copy-start | bytes 3076
  161.5 83.7 %copy-start.47 = (f32[128]{0:T(128)}, f32[128]{0:T(128)S(1)}, u32[]{:S(2)}) copy-start(f32[128]{0:T(128)S(1)} %get-tuple-element.154) | copy-start | bytes 1540
  161.5 83.7 %copy-start.54 = (f32[128]{0:T(128)}, f32[128]{0:T(128)S(1)}, u32[]{:S(2)}) copy-start(f32[128]{0:T(128)S(1)} %get-tuple-element.153) | copy-start | bytes 1540
  161.5 83.7 %copy-start.58 = (f32[128]{0:T(128)}, f32[128]{0:T(128)S(1)}, u32[]{:S(2)}) copy-start(f32[128]{0:T(128)S(1)} %get-tuple-element.152) | copy-start | bytes 1540
  194.4 50.8 %copy-start.15 = (f32[256,128]{1,0:T(8,128)}, f32[256,128]{1,0:T(8,128)S(1)}, u32[]{:S(2)}) copy-start(f32[256,128]{1,0:T(8,128)S(1)} %get-tuple-element.144) | copy-start | bytes 393220
  249.6 165.9 %reduce-scatter.12.cloned.1.call-start = ((), (), s32[]{:S(2)}) async-start(), calls=%async_computation.9 | async-start | bytes 5242880
  371.0 123.2 %all-gather.8.cloned.1.call-start = ((), (), s32[]{:S(2)}) async-start(), calls=%async_computation.7 | async-start | bytes 5242880 | tf_op jit(solution)/shard_map/all_gather | solution.py:116
  376.3 208.3 %reduce-scatter.14.cloned.1.call-start = ((), (), s32[]{:S(2)}) async-start(), calls=%async_computation.10 | async-start | bytes 5242880
  501.9 20.2 %all-to-all-start.1 = ((bf16[8,144,2,128]{3,2,1,0:T(2,128)(2,1)}), bf16[8,144,2,128]{3,2,1,0:T(2,128)(2,1)S(1)}, u32[]{:S(2)}, u32[]{:S(2)}) async-start(bf16[8,144,2,128]{3,2,1,0:T(2,128)(2,1)} %convert_element_type.186), calls=%async_computation.1 | async-start | bytes 1179648 | tf_op jit(solution)/shard_map/all_to_all | solution.py:29
  522.2 58.7 %all-to-all-start = ((bf16[8,64,1792]{2,1,0:T(8,128)(2,1)}), bf16[8,64,1792]{2,1,0:T(8,128)(2,1)S(1)}, u32[]{:S(2)}, u32[]{:S(2)}) async-start(bf16[8,64,1792]{2,1,0:T(8,128)(2,1)} %pad_maximum_fusion.4), calls=%async_computation | async-start | bytes 3670016 | tf_op jit(solution)/shard_map/all_to_all | solution.py:29
  540.0 38.3 %copy-start.46 = (f32[10,128]{1,0:T(8,128)S(1)}, f32[10,128]{1,0:T(8,128)}, u32[]{:S(2)}) copy-start(f32[10,128]{1,0:T(8,128)} %param.42) | copy-start | bytes 15364
  540.0 38.3 %copy-start.56 = (f32[10,128]{1,0:T(8,128)S(1)}, f32[10,128]{1,0:T(8,128)}, u32[]{:S(2)}) copy-start(f32[10,128]{1,0:T(8,128)} %param.44) | copy-start | bytes 15364
  540.0 38.3 %copy-start.57 = (f32[10,128]{1,0:T(8,128)S(1)}, f32[10,128]{1,0:T(8,128)}, u32[]{:S(2)}) copy-start(f32[10,128]{1,0:T(8,128)} %param.43) | copy-start | bytes 15364
  540.2 39.3 %copy-start.24 = (f32[144,2,128]{2,1,0:T(2,128)S(1)}, f32[144,2,128]{2,1,0:T(2,128)}, u32[]{:S(2)}) copy-start(f32[144,2,128]{2,1,0:T(2,128)} %param.39) | copy-start | bytes 442372
  540.2 39.3 %copy-start.35 = (f32[144,2,128]{2,1,0:T(2,128)S(1)}, f32[144,2,128]{2,1,0:T(2,128)}, u32[]{:S(2)}) copy-start(f32[144,2,128]{2,1,0:T(2,128)} %param.41) | copy-start | bytes 442372
  540.2 39.3 %copy-start.36 = (f32[144,2,128]{2,1,0:T(2,128)S(1)}, f32[144,2,128]{2,1,0:T(2,128)}, u32[]{:S(2)}) copy-start(f32[144,2,128]{2,1,0:T(2,128)} %param.40) | copy-start | bytes 442372
  542.0 39.1 %copy-start.38 = (f32[64,128]{1,0:T(8,128)S(1)}, f32[64,128]{1,0:T(8,128)}, u32[]{:S(2)}) copy-start(f32[64,128]{1,0:T(8,128)} %param.33) | copy-start | bytes 98308
  542.0 39.1 %copy-start.44 = (f32[64,128]{1,0:T(8,128)S(1)}, f32[64,128]{1,0:T(8,128)}, u32[]{:S(2)}) copy-start(f32[64,128]{1,0:T(8,128)} %param.35) | copy-start | bytes 98308
  (53 other events, 204.2 us)
Sparse Core Ops, SparseCore 0:
  11.5 36.1 all-gather.3
  59.6 48.1 reduce-scatter.9
  249.7 34.2 all-gather.5
  371.1 44.2 reduce-scatter.11
  417.5 34.4 all-gather.7
  464.1 44.5 reduce-scatter.13
where the time goes:
time: 606 us; the launch traced here: 595 us
  blocking collectives  227 us (37%)
  local copies, waits for them, and re-layouts  173 us (29%)
  other arithmetic  67.5 us (11%)
  matrix products  55.8 us (9%)
  waiting for transfers between devices  44.4 us (7%)
  between operations  16 us (3%)
  starting transfers between devices  11.6 us (2%)
    unnamed x155, local copies, waits for them, and re-layouts  61.1 us
    unnamed x9, waiting for transfers between devices  39.3 us
    pmax x1, blocking collectives, body(): lax.pmax((jnp.max(condition, axis=0), -jnp.min(condition, axis=0)), 'dp')  37.5 us
    psum x1, blocking collectives, body(): small_total = lax.psum(small_grad, 'dp')  36.2 us
    all_gather x1, blocking collectives, body(): lax.all_gather(film_w.astype(low_type), 'dp', axis=0, tiled=True)  31.5 us
    all_gather x1, blocking collectives, body(): lax.all_gather(conv2_w.astype(low_type), 'dp', axis=0, tiled=True)  31.5 us
    all_gather x1, blocking collectives, body(): lax.all_gather(conv1_w.astype(low_type), 'dp', axis=0, tiled=True)  31.4 us
    all_gather x1, blocking collectives, body(): lax.all_gather(res_w.astype(low_type), 'dp', axis=0, tiled=True)  30.5 us
  transfers between devices with their start and end apart: 8, of which 2 were waited for; matrix products, arithmetic and copies ran while one was open for 33% of the time, Pallas kernels for 0%

commit v1 on v0

v1 whole, which is shorter than its diff:
```python
from functools import partial

import jax
import jax.numpy as jnp
from jax import lax
from jax.experimental import pallas as pl
from jax.experimental.pallas import tpu as pltpu
from jax.sharding import PartitionSpec as P

f32, bf16 = jnp.float32, jnp.bfloat16
GROUP = 64
TAPS = 5
DOWN = 3
eps_norm = 1e-05


def dot_nn(a, b):
    return lax.dot_general(a, b, (((1,), (0,)), ((), ())), preferred_element_type=f32)


def dot_nt(a, b):
    return lax.dot_general(a, b, (((1,), (1,)), ((), ())), preferred_element_type=f32)


def dot_tn(a, b):
    return lax.dot_general(a, b, (((0,), (0,)), ((), ())), preferred_element_type=f32)


def mish_pair(v):
    u = jnp.exp(-jnp.abs(v))
    pos = v >= 0
    num = jnp.where(pos, 1.0 + 2.0 * u, u * (u + 2.0))
    q = jnp.where(pos, 2.0 * u * u, 2.0)
    r = 1.0 / (num + q)
    w = num * r
    sig = jnp.where(pos, 1.0, u) / (1.0 + u)
    return v * w, w + v * sig * ((q * r) * ((2.0 * num + q) * r))


def wide(tile, lanes):
    return jnp.concatenate([tile] * (lanes // tile.shape[1]), axis=1)


def grid_turn(outer, inner):
    n = outer * inner
    row = lax.broadcasted_iota(jnp.int32, (n, n), 0)
    col = lax.broadcasted_iota(jnp.int32, (n, n), 1)
    return ((row % outer) * inner + row // outer == col).astype(bf16)


def group_sum(values):
    s, c = values.shape
    row = lax.broadcasted_iota(jnp.int32, (128, 128), 0)
    col = lax.broadcasted_iota(jnp.int32, (128, 128), 1)
    ones = (row // GROUP == col // GROUP).astype(f32)
    tall = jnp.concatenate([values[:, i : i + 128] for i in range(0, c, 128)], axis=0)
    tot = lax.dot_general(tall, ones, (((1,), (0,)), ((), ())), precision=lax.Precision.HIGHEST, preferred_element_type=f32)
    return jnp.concatenate([tot[i * s : (i + 1) * s] for i in range(c // 128)], axis=1)


MESH = pl.DeviceIdType.MESH
PARTS = ((0, TAPS + 1), (TAPS + 1, TAPS), (2 * TAPS + 1, DOWN))
SMALL = 16


def step_kernel(
    n_dp, n_ch,
    inputs, cot, cond, lens_all, one_w, two_w, res_w, down_w, film_w, small_w,
    output, input_grad, gfin, gffin, gsfin,
    w_all, gw_all, x_raw, cot_raw, out_raw, ig_raw, small, stats, act, wf_all, film_out, film, gfilm, gfa, gwf,
    rcb, rxb, ryb, rzb, rfx, rfz, gsm, gsr,
    xpad, hpad, be, bo, cbuf, res, xh1, m1, dm1, xh2, dm2, gdn, gc2, gc1, gres,
    ag_send, ag_recv, st_send, st_recv, in_send, in_recv, fw_send, fw_recv, fo_send, fo_recv,
    rs_send, rs_recv, rz_send, rz_recv, out_send, out_recv, gf_send, gf_recv, rf_send, rf_recv, gs_send, gs_recv, loc,
):
    dp, ch = lax.axis_index("dp"), lax.axis_index("chan")
    hi, lo, yy, co = dp // 2, dp % 2, ch // 2, ch % 2
    n_hi = n_dp // 2
    dp_x = hi * 2 + 1 - lo
    ch_y = (1 - yy) * 2 + co
    ch_c = yy * 2 + 1 - co
    m, c = x_raw.shape
    h2 = m // 2
    rows, width = res_w.shape
    frp = film_w.shape[0]
    s = m // (inputs.shape[0] // lens_all.shape[0])
    frames = m // s
    half = frames // 2
    MC = 256 if m % 256 == 0 else m
    NB = 256

    def at(index, size):
        return pl.ds(pl.multiple_of(index * size, size), size)

    def remote(src, dst, ss, rs, device):
        return pltpu.make_async_remote_copy(
            src_ref=src, dst_ref=dst, send_sem=ss, recv_sem=rs, device_id=device, device_id_type=MESH
        )

    barrier = pltpu.get_barrier_semaphore()

    @pl.loop(1, n_dp)
    def _(i):
        pl.semaphore_signal(barrier, inc=1, device_id=((dp + i) % n_dp, ch), device_id_type=MESH)

    for i in range(1, n_ch):
        pl.semaphore_signal(barrier, inc=1, device_id=(dp, (ch + i) % n_ch), device_id_type=MESH)

    own_x = pltpu.make_async_copy(inputs.at[at(ch, m)], x_raw.at[:, at(ch, width)], loc.at[0])
    own_x.start()
    own_cot = pltpu.make_async_copy(cot.at[at(ch, h2)], cot_raw.at[:, at(ch, width)], loc.at[1])
    own_cot.start()
    my_rows, my_cols = at(dp, rows), at(ch, width)
    for k in range(TAPS):
        w_all[k, my_rows, my_cols] = one_w[:, k, :].astype(bf16)
    w_all[TAPS, my_rows, my_cols] = res_w[...].astype(bf16)
    for k in range(TAPS):
        w_all[TAPS + 1 + k, my_rows, my_cols] = two_w[:, k, :].astype(bf16)
    for k in range(DOWN):
        w_all[2 * TAPS + 1 + k, my_rows, my_cols] = down_w[:, k, :].astype(bf16)
    for i in range(2):
        wf_all[i, at(dp, frp), :] = film_w[:, i, :].astype(bf16)
    small[pl.ds(0, small_w.shape[0]), my_cols] = small_w[...]
    small[pl.ds(small_w.shape[0], SMALL - small_w.shape[0]), my_cols] = jnp.zeros((SMALL - small_w.shape[0], width), f32)
    values = cond[...]
    stats[dp, pl.ds(0, 1), :] = jnp.max(values, axis=0, keepdims=True)
    stats[dp, pl.ds(1, 1), :] = -jnp.min(values, axis=0, keepdims=True)
    stats[dp, pl.ds(2, 6), :] = jnp.zeros((6, values.shape[1]), f32)
    pad0 = jnp.zeros((2 * s, c), bf16)
    for ref in (xpad, hpad, gc2, gc1):
        ref[pl.ds(0, 2 * s), :] = pad0
        ref[pl.ds((frames + 2) * s, 2 * s), :] = pad0
    bo[pl.ds(0, s), :] = pad0[:s]
    gdn[pl.ds(half * s, s), :] = pad0[:s]
    pl.semaphore_wait(barrier, n_dp - 1 + n_ch - 1)

    def block(p, d, q):
        t0, nt = PARTS[p]
        return w_all.at[pl.ds(t0, nt), at(d, rows), at(q, width)]

    def pass_on(p, d, q, slot, device):
        return remote(block(p, d, q), block(p, d, q), ag_send.at[p, slot], ag_recv.at[p, d, q], device)

    def to_y(p, h):
        return pass_on(p, h * 2 + lo, ch, n_hi + h, (dp, ch_y))

    def to_x(p, h, v):
        return pass_on(p, h * 2 + lo, v * 2 + co, 2 * n_hi + 2 * h + v, (dp_x, ch))

    def to_c(p, h, l, v):
        return pass_on(p, h * 2 + l, v * 2 + co, 4 * n_hi + 4 * h + 2 * l + v, (dp, ch_c))

    def to_z(p, i):
        return pass_on(p, dp, ch, i, ((hi + i) % n_hi * 2 + lo, ch))

    def landed(p, d, q):
        pass_on(p, d, q, 0, (dp, ch)).wait_recv()

    def ag_own(p):
        @pl.loop(1, n_hi)
        def _(i):
            to_z(p, i).start()

        to_y(p, hi).start()
        to_x(p, hi, yy).start()
        to_c(p, hi, lo, yy).start()

    def ag_z(p):
        @pl.loop(1, n_hi)
        def _(i):
            h = (hi + i) % n_hi
            landed(p, h * 2 + lo, ch)
            to_y(p, h).start()
            to_x(p, h, yy).start()
            to_c(p, h, lo, yy).start()

    def ag_y(p):
        @pl.loop(0, n_hi)
        def _(i):
            h = (hi + i) % n_hi
            landed(p, h * 2 + lo, ch_y)
            to_x(p, h, 1 - yy).start()
            to_c(p, h, lo, 1 - yy).start()

    def ag_x(p):
        @pl.loop(0, n_hi)
        def _(i):
            h = (hi + i) % n_hi
            landed(p, h * 2 + 1 - lo, ch)
            to_c(p, h, 1 - lo, yy).start()

        @pl.loop(0, n_hi)
        def _(i):
            h = (hi + i) % n_hi
            landed(p, h * 2 + 1 - lo, ch_y)
            to_c(p, h, 1 - lo, 1 - yy).start()

    def ag_core(p):
        @pl.loop(0, n_dp)
        def _(d):
            for v in range(n_ch // 2):
                landed(p, d, v * 2 + 1 - co)

    def ag_done(p):
        @pl.loop(1, n_hi)
        def _(i):
            to_z(p, i).wait_send()

        @pl.loop(0, n_hi)
        def _(h):
            to_y(p, h).wait_send()
            for v in range(2):
                to_x(p, h, v).wait_send()
                for l in range(2):
                    to_c(p, h, l, v).wait_send()

    def swap_in(src, dst, n, k, i):
        q = (ch + i) % n_ch
        return remote(src.at[at(q, n)], dst.at[:, my_cols], in_send.at[k, i], in_recv.at[k, i], (dp, q))

    def swap_in_wait(src, dst, n, k):
        for i in range(1, n_ch):
            q = (ch + n_ch - i) % n_ch
            remote(src.at[at(q, n)], dst.at[:, at(q, width)], in_send.at[k, i], in_recv.at[k, i], (dp, q)).wait_recv()
        for i in range(1, n_ch):
            swap_in(src, dst, n, k, i).wait_send()

    def swap_out(src, dst, n, k, i):
        q = (ch + i) % n_ch
        return remote(src.at[:, at(q, width)], dst.at[at(ch, n)], out_send.at[k, i], out_recv.at[k, i], (dp, q))

    def swap_out_wait(src, dst, n, k):
        for i in range(1, n_ch):
            q = (ch + n_ch - i) % n_ch
            remote(src.at[:, at(q, width)], dst.at[at(q, n)], out_send.at[k, i], out_recv.at[k, i], (dp, q)).wait_recv()
        for i in range(1, n_ch):
            swap_out(src, dst, n, k, i).wait_send()

    def small_swap(i, q):
        return remote(small.at[:, at(q, width)], small.at[:, at(q, width)], in_send.at[2, i], in_recv.at[2, i], (dp, (ch + i) % n_ch))

    def bounds(i, d):
        return remote(stats.at[d], stats.at[d], st_send.at[i], st_recv.at[i], ((dp + i) % n_dp, ch))

    def film_block(d):
        return wf_all.at[:, at(d, frp), :]

    def film_pass(d, slot, device):
        return remote(film_block(d), film_block(d), fw_send.at[slot], fw_recv.at[d], device)

    def film_z(i):
        return film_pass(dp, i, ((hi + i) % n_hi * 2 + lo, ch))

    def film_x(h):
        return film_pass(h * 2 + lo, n_hi + h, (dp_x, ch))

    def film_swap(i, q):
        return remote(
            film_out.at[:, at(q, s), :], film.at[:, :, my_cols], fo_send.at[i], fo_recv.at[i], (dp, q)
        )

    @pl.loop(1, n_dp)
    def _(i):
        bounds(i, dp).start()

    ag_own(0)
    for i in range(1, n_ch):
        small_swap(i, ch).start()
        swap_in(inputs, x_raw, m, 0, i).start()

    @pl.loop(1, n_hi)
    def _(i):
        film_z(i).start()

    ag_z(0)
    film_x(hi).start()
    ag_y(0)

    @pl.loop(1, n_hi)
    def _(i):
        h = (hi + i) % n_hi
        film_pass(h * 2 + lo, 0, (dp, ch)).wait_recv()
        film_x(h).start()

    ag_own(1)
    ag_x(0)

    @pl.loop(1, n_dp)
    def _(i):
        bounds(i, (dp + n_dp - i) % n_dp).wait_recv()

    def widest(d, best):
        return jnp.maximum(best, stats[d])

    best = lax.fori_loop(1, n_dp, widest, stats[0])
    low = -best[1:2, :]
    span = jnp.maximum(best[0:1, :] - low, 1.0)
    CB = 64

    @pl.loop(0, cond.shape[0] // CB)
    def _(i):
        v = 2.0 * (cond[at(i, CB), :] - low) / span - 1.0
        act[at(i, CB), :] = mish_pair(v)[0].astype(bf16)

    ag_z(1)

    @pl.loop(0, n_hi)
    def _(h):
        film_pass(h * 2 + 1 - lo, 0, (dp, ch)).wait_recv()

    for i in range(2):
        film_out[i] = dot_nn(act[...], wf_all[i]) + small[pl.ds(6 + i, 1), my_cols]
    for i in range(1, n_ch):
        film_swap(i, (ch + i) % n_ch).start()
    for i in range(2):
        film[i, :, my_cols] = film_out[i, at(ch, s), :]

    lens_ref = lens_all.at[at(ch, s)]

    def mask(t):
        return wide((lens_ref[...] > t).astype(f32), c)

    count = wide(lens_ref[...].astype(f32), c) * GROUP
    own_x.wait()
    swap_in_wait(inputs, x_raw, m, 0)
    sb = 256 // frames
    turn = grid_turn(sb, frames)
    for b in range(s // sb):
        y = dot_nn(turn, x_raw[pl.ds(b * 256, 256), :])
        lens_b = lens_ref[pl.ds(b * sb, sb), :]
        for t in range(frames):
            keep = wide((lens_b > t).astype(f32), c)
            xpad[pl.ds((t + 2) * s + b * sb, sb), :] = (y[t * sb : (t + 1) * sb] * keep).astype(bf16)

    def conv_fwd(src, base, store):
        @pl.loop(0, c // NB)
        def _(n):
            cols = at(n, NB)
            for mi in range(m // MC):
                acc = dot_nn(src[pl.ds(mi * MC, MC), :], w_all[base, :, cols])
                for k in range(1, TAPS):
                    acc += dot_nn(src[pl.ds(mi * MC + k * s, MC), :], w_all[base + k, :, cols])
                store(pl.ds(mi * MC, MC), cols, acc)

    def conv_bwd(src, base, store):
        @pl.loop(0, c // NB)
        def _(n):
            cols = at(n, NB)
            for mi in range(m // MC):
                acc = dot_nt(src[pl.ds(mi * MC + (TAPS - 1) * s, MC), :], w_all[base, cols, :])
                for k in range(1, TAPS):
                    acc += dot_nt(src[pl.ds(mi * MC + (TAPS - 1 - k) * s, MC), :], w_all[base + k, cols, :])
                store(pl.ds(mi * MC, MC), cols, acc)

    def conv_grad(src, g, base):
        @pl.loop(0, TAPS)
        def _(k):
            shifted = pl.ds(pl.multiple_of((TAPS - 1 - k) * s, s), m)
            for n in range(c // NB):
                cols = pl.ds(n * NB, NB)
                gw_all[base + k, :, cols] = dot_tn(src[pl.ds(2 * s, m), :], g[shifted, cols]).astype(bf16)

    def norm_stats(bias):
        tot = jnp.zeros((s, c), f32)
        for t in range(frames):
            tot += (cbuf[pl.ds(t * s, s), :] + bias) * mask(t)
        mean = group_sum(tot) / count
        tot = jnp.zeros((s, c), f32)
        for t in range(frames):
            d = (cbuf[pl.ds(t * s, s), :] + bias - mean) * mask(t)
            tot += d * d
        return mean, lax.rsqrt(group_sum(tot) / count + eps_norm)

    def row(i):
        return small[pl.ds(i, 1), :]

    def keep_c(part, cols, acc):
        cbuf[part, cols] = acc

    ag_core(0)
    conv_fwd(xpad, 0, keep_c)
    ag_y(1)
    for n in range(c // NB):
        cols = pl.ds(n * NB, NB)
        for mi in range(m // MC):
            res[pl.ds(mi * MC, MC), cols] = dot_nn(xpad[pl.ds(2 * s + mi * MC, MC), :], w_all[TAPS, :, cols])
    ag_own(2)
    for i in range(1, n_ch):
        swap_in(cot, cot_raw, h2, 1, i).start()
    ag_x(1)
    for i in range(1, n_ch):
        small_swap(i, (ch + n_ch - i) % n_ch).wait_recv()
        q = (ch + n_ch - i) % n_ch
        remote(film_out.at[:, at(q, s), :], film.at[:, :, at(q, width)], fo_send.at[i], fo_recv.at[i], (dp, q)).wait_recv()
    bias = row(0)
    mean, rstd1 = norm_stats(bias)
    ag_z(2)
    for t in range(frames):
        part = pl.ds(t * s, s)
        xh = (cbuf[part, :] + bias - mean) * rstd1
        mi, dmi = mish_pair(xh * row(1) + row(2))
        xh1[part, :] = xh
        m1[part, :] = mi
        dm1[part, :] = dmi
        hpad[pl.ds((t + 2) * s, s), :] = ((film[0] * mi + film[1]) * mask(t)).astype(bf16)
    ag_y(2)
    ag_core(1)
    conv_fwd(hpad, TAPS + 1, keep_c)
    ag_x(2)
    bias = row(3)
    mean, rstd2 = norm_stats(bias)
    for t in range(frames):
        part = pl.ds(t * s, s)
        xh = (cbuf[part, :] + bias - mean) * rstd2
        mi, dmi = mish_pair(xh * row(4) + row(5))
        xh2[part, :] = xh
        dm2[part, :] = dmi
        val = ((mi + res[part, :] + row(8)) * mask(t)).astype(bf16)
        if t % 2 == 0:
            be[pl.ds(t // 2 * s, s), :] = val
        else:
            bo[pl.ds((t // 2 + 1) * s, s), :] = val
    own_cot.wait()
    swap_in_wait(cot, cot_raw, h2, 1)
    sh = 256 // half
    turn_h = grid_turn(sh, half)
    for b in range(s // sh):
        y = dot_nn(turn_h, cot_raw[pl.ds(b * 256, 256), :])
        lens_b = lens_ref[pl.ds(b * sh, sh), :]
        for j in range(half):
            keep = wide((lens_b > 2 * j).astype(f32), c)
            gdn[pl.ds(j * s + b * sh, sh), :] = (y[j * sh : (j + 1) * sh] * keep).astype(bf16)

    def rs_core(p, v):
        t0, nt = PARTS[p]
        return remote(
            gw_all.at[pl.ds(t0, nt), :, at(v * 2 + 1 - co, width)],
            rcb.at[pl.ds(t0, nt), :, pl.ds(v * width, width)],
            rs_send.at[p, v], rs_recv.at[p, v], (dp, ch_c),
        )

    def rs_x(p, h):
        t0, nt = PARTS[p]
        return remote(
            rcb.at[pl.ds(t0, nt), at(h * 2 + 1 - lo, rows), :],
            rxb.at[pl.ds(t0, nt), at(h, rows), :],
            rz_send.at[p, n_hi + h], rz_recv.at[p, n_hi + h], (dp_x, ch),
        )

    def rs_y(p):
        t0, nt = PARTS[p]
        return remote(
            rxb.at[pl.ds(t0, nt), :, at(1 - yy, width)], ryb.at[pl.ds(t0, nt)], rs_send.at[p, 2], rs_recv.at[p, 2], (dp, ch_y)
        )

    def rs_z(p, i):
        t0, nt = PARTS[p]
        h = (hi + i) % n_hi
        return remote(
            ryb.at[pl.ds(t0, nt), at(h, rows), :], rzb.at[i, pl.ds(t0, nt)], rz_send.at[p, i], rz_recv.at[p, i], (h * 2 + lo, ch)
        )

    def rs_start(p):
        for v in range(2):
            rs_core(p, v).start()

    def rs_after_core(p):
        t0, nt = PARTS[p]
        for v in range(2):
            rs_core(p, v).wait()

        @pl.loop(t0, t0 + nt)
        def _(k):
            for v in range(2):
                cols = pl.ds(v * width, width)
                rcb[k, :, cols] = (rcb[k, :, cols].astype(f32) + gw_all[k, :, at(v * 2 + co, width)].astype(f32)).astype(bf16)

        @pl.loop(0, n_hi)
        def _(h):
            rs_x(p, h).start()

    def rs_after_x(p):
        t0, nt = PARTS[p]

        @pl.loop(0, n_hi)
        def _(h):
            rs_x(p, h).wait()

        @pl.loop(t0, t0 + nt)
        def _(k):
            @pl.loop(0, n_hi)
            def _(h):
                part = at(h, rows)
                rxb[k, part, :] = (rxb[k, part, :].astype(f32) + rcb[k, at(h * 2 + lo, rows), :].astype(f32)).astype(bf16)

        rs_y(p).start()

    def rs_after_y(p):
        t0, nt = PARTS[p]
        rs_y(p).wait()

        @pl.loop(t0, t0 + nt)
        def _(k):
            ryb[k] = (ryb[k].astype(f32) + rxb[k, :, at(yy, width)].astype(f32)).astype(bf16)

        @pl.loop(1, n_hi)
        def _(i):
            rs_z(p, i).start()

    def rs_after_z(p):
        t0, nt = PARTS[p]

        @pl.loop(1, n_hi)
        def _(i):
            rs_z(p, i).wait()

        @pl.loop(t0, t0 + nt)
        def _(k):
            def more(i, tot):
                return tot + rzb[i, k].astype(f32)

            gfin[k] = lax.fori_loop(1, n_hi, more, ryb[k, at(hi, rows), :].astype(f32))

    ag_core(2)
    hm = half * s
    back_h = grid_turn(half, sh)
    dbase = 2 * TAPS + 1
    taps_in = (bo, be, bo)
    taps_at = (0, 0, s)
    for k in range(DOWN):
        for n in range(c // NB):
            cols = pl.ds(n * NB, NB)
            gw_all[dbase + k, :, cols] = dot_tn(taps_in[k][pl.ds(taps_at[k], hm), :], gdn[pl.ds(0, hm), cols]).astype(bf16)
    rs_start(2)
    for n in range(c // NB):
        cols = pl.ds(n * NB, NB)
        acc = dot_nn(bo[pl.ds(0, hm), :], w_all[dbase, :, cols])
        acc += dot_nn(be[...], w_all[dbase + 1, :, cols])
        acc += dot_nn(bo[pl.ds(s, hm), :], w_all[dbase + 2, :, cols])
        cbuf[pl.ds(0, hm), cols] = acc
    for b in range(s // sh):
        pieces = []
        lens_b = lens_ref[pl.ds(b * sh, sh), :]
        for j in range(half):
            keep = wide((lens_b > 2 * j).astype(f32), c)
            pieces.append(((cbuf[pl.ds(j * s + b * sh, sh), :] + row(9)) * keep).astype(bf16))
        out_raw[pl.ds(b * 256, 256), :] = dot_nn(back_h, jnp.concatenate(pieces, axis=0)).astype(bf16)
    rs_after_core(2)
    for i in range(1, n_ch):
        swap_out(out_raw, output, h2, 0, i).start()
    own_out = pltpu.make_async_copy(out_raw.at[:, my_cols], output.at[at(ch, h2)], loc.at[2])
    own_out.start()

    tot = jnp.zeros((s, c), f32)
    for j in range(half):
        tot += gdn[pl.ds(j * s, s), :].astype(f32)
    gs = [None] * SMALL
    gs[9] = jnp.sum(tot, axis=0, keepdims=True)
    for n in range(c // NB):
        cols = pl.ds(n * NB, NB)
        ge = dot_nt(gdn[pl.ds(0, hm), :], w_all[dbase + 1, cols, :])
        go = dot_nt(gdn[pl.ds(0, hm), :], w_all[dbase + 2, cols, :])
        go += dot_nt(gdn[pl.ds(s, hm), :], w_all[dbase, cols, :])
        for j in range(half):
            cbuf[pl.ds(2 * j * s, s), cols] = ge[j * s : (j + 1) * s]
            cbuf[pl.ds((2 * j + 1) * s, s), cols] = go[j * s : (j + 1) * s]

    def norm_back(xh, dm, gain, rstd, dst, scale):
        a1 = jnp.zeros((s, c), f32)
        a2 = jnp.zeros((s, c), f32)
        for t in range(frames):
            part = pl.ds(t * s, s)
            dy = cbuf[part, :] * mask(t) * dm[part, :]
            if scale is not None:
                dy = dy * scale
            dm[part, :] = dy
            a1 += dy
            a2 += dy * xh[part, :]
        g1 = group_sum(a1 * gain) / count
        g2 = group_sum(a2 * gain) / count
        tot = jnp.zeros((s, c), f32)
        for t in range(frames):
            part = pl.ds(t * s, s)
            dp_t = rstd * (dm[part, :] * gain - mask(t) * (g1 + xh[part, :] * g2))
            tot += dp_t
            dst[pl.ds((t + 2) * s, s), :] = dp_t.astype(bf16)
        return [jnp.sum(v, axis=0, keepdims=True) for v in (tot, a2, a1)]

    tot = jnp.zeros((s, c), f32)
    for t in range(frames):
        part = pl.ds(t * s, s)
        g = cbuf[part, :] * mask(t)
        tot += g
        gres[part, :] = g.astype(bf16)
    gs[8] = jnp.sum(tot, axis=0, keepdims=True)
    gs[3:6] = norm_back(xh2, dm2, row(4), rstd2, gc2, None)
    conv_grad(hpad, gc2, TAPS + 1)
    rs_start(1)
    rs_after_x(2)
    conv_bwd(gc2, TAPS + 1, keep_c)
    rs_after_core(1)
    rs_after_y(2)
    tot1 = jnp.zeros((s, c), f32)
    tot2 = jnp.zeros((s, c), f32)
    for t in range(frames):
        part = pl.ds(t * s, s)
        g = cbuf[part, :] * mask(t)
        tot1 += g * m1[part, :]
        tot2 += g
    gfilm[0] = tot1.astype(bf16)
    gfilm[1] = tot2.astype(bf16)
    gs[6] = jnp.sum(tot1, axis=0, keepdims=True)
    gs[7] = jnp.sum(tot2, axis=0, keepdims=True)

    def film_back(i):
        q = (ch + i) % n_ch
        return remote(gfilm.at[:, :, at(q, width)], gfa.at[:, at(ch, s), :], gf_send.at[i], gf_recv.at[i], (dp, q))

    for i in range(1, n_ch):
        film_back(i).start()
    gfa[:, at(ch, s), :] = gfilm[:, :, my_cols]
    gs[0:3] = norm_back(xh1, dm1, row(1), rstd1, gc1, film[0])
    conv_grad(xpad, gc1, 0)
    for n in range(c // NB):
        cols = pl.ds(n * NB, NB)
        gw_all[TAPS, :, cols] = dot_tn(xpad[pl.ds(2 * s, m), :], gres[:, cols]).astype(bf16)
    rs_start(0)
    zero = jnp.zeros((1, c), f32)
    for i in range(SMALL):
        gsm[pl.ds(i, 1), :] = gs[i] if gs[i] is not None else zero

    def small_pass(i, device):
        return remote(gsm, gsr.at[i], gs_send.at[i], gs_recv.at[i], device)

    small_pass(0, (dp, ch_c)).start()

    def keep_ig(part, cols, acc):
        cbuf[part, cols] = acc + dot_nt(gres[part, :], w_all[TAPS, cols, :])

    conv_bwd(gc1, 0, keep_ig)
    rs_after_x(1)
    rs_after_core(0)
    back = grid_turn(frames, sb)
    for b in range(s // sb):
        lens_b = lens_ref[pl.ds(b * sb, sb), :]
        pieces = [
            (cbuf[pl.ds(t * s + b * sb, sb), :] * wide((lens_b > t).astype(f32), c)).astype(bf16) for t in range(frames)
        ]
        ig_raw[pl.ds(b * 256, 256), :] = dot_nn(back, jnp.concatenate(pieces, axis=0)).astype(bf16)
    for i in range(1, n_ch):
        swap_out(ig_raw, input_grad, m, 1, i).start()
    own_ig = pltpu.make_async_copy(ig_raw.at[:, my_cols], input_grad.at[at(ch, m)], loc.at[3])
    own_ig.start()

    for i in range(1, n_ch):
        q = (ch + n_ch - i) % n_ch
        remote(gfilm.at[:, :, at(q, width)], gfa.at[:, at(q, s), :], gf_send.at[i], gf_recv.at[i], (dp, q)).wait_recv()
    for i in range(2):
        gwf[i] = dot_tn(act[...], gfa[i]).astype(bf16)

    def rf_x(h):
        return remote(gwf.at[:, at(h * 2 + 1 - lo, frp), :], rfx.at[:, at(h, frp), :], rf_send.at[n_hi + h], rf_recv.at[n_hi + h], (dp_x, ch))

    def rf_z(i):
        h = (hi + i) % n_hi
        return remote(rfx.at[:, at(h, frp), :], rfz.at[i], rf_send.at[i], rf_recv.at[i], (h * 2 + lo, ch))

    @pl.loop(0, n_hi)
    def _(h):
        rf_x(h).start()

    small_pass(0, (dp, ch_c)).wait()
    gsm[...] += gsr[0]
    small_pass(1, (dp_x, ch)).start()
    rs_after_z(2)
    rs_after_y(1)
    small_pass(1, (dp_x, ch)).wait()
    gsm[...] += gsr[1]
    small_pass(2, (dp, ch_y)).start()

    @pl.loop(0, n_hi)
    def _(h):
        rf_x(h).wait()

    for i in range(2):
        @pl.loop(0, n_hi)
        def _(h):
            part = at(h, frp)
            rfx[i, part, :] = (rfx[i, part, :].astype(f32) + gwf[i, at(h * 2 + lo, frp), :].astype(f32)).astype(bf16)

    @pl.loop(1, n_hi)
    def _(i):
        rf_z(i).start()

    small_pass(2, (dp, ch_y)).wait()
    gsm[...] += gsr[2]

    def small_z(i):
        return small_pass(2 + i, ((hi + i) % n_hi * 2 + lo, ch))

    @pl.loop(1, n_hi)
    def _(i):
        small_z(i).start()

    rs_after_z(1)

    @pl.loop(1, n_hi)
    def _(i):
        rf_z(i).wait()

    for v in range(2):
        def more(i, tot):
            return tot + rfz[i, v].astype(f32)

        gffin[v] = lax.fori_loop(1, n_hi, more, rfx[v, at(hi, frp), :].astype(f32))

    @pl.loop(1, n_hi)
    def _(i):
        small_z(i).wait()

    def more_small(i, tot):
        return tot + gsr[2 + i, :, my_cols]

    gsfin[...] = lax.fori_loop(1, n_hi, more_small, gsm[:, my_cols])
    rs_after_x(0)
    rs_after_y(0)
    rs_after_z(0)

    own_out.wait()
    own_ig.wait()
    swap_out_wait(out_raw, output, h2, 0)
    swap_out_wait(ig_raw, input_grad, m, 1)
    for p in range(3):
        ag_done(p)

    @pl.loop(1, n_dp)
    def _(i):
        bounds(i, dp).wait_send()

    @pl.loop(1, n_hi)
    def _(i):
        film_z(i).wait_send()

    @pl.loop(0, n_hi)
    def _(h):
        film_x(h).wait_send()

    for i in range(1, n_ch):
        small_swap(i, ch).wait_send()
        film_swap(i, (ch + i) % n_ch).wait_send()
        film_back(i).wait_send()


def block_step(n_dp, n_ch, inputs, cot, cond, lens_all, one_w, two_w, res_w, down_w, film_w, small_w):
    rows, width = res_w.shape
    c = rows * n_dp
    samples = lens_all.shape[0]
    s = samples // n_ch
    m = inputs.shape[0] // n_ch
    h = m // 2
    frp = film_w.shape[0]
    feats = cond.shape[1]
    n_hi = n_dp // 2
    taps = 2 * TAPS + 1 + DOWN
    V = pltpu.VMEM
    D = pltpu.SemaphoreType.DMA
    vm = pl.BlockSpec(memory_space=pltpu.VMEM)
    hbm = pl.BlockSpec(memory_space=pl.ANY)
    out = [
        jax.ShapeDtypeStruct((h * n_ch, width), bf16),
        jax.ShapeDtypeStruct((m * n_ch, width), bf16),
        jax.ShapeDtypeStruct((taps, rows, width), f32),
        jax.ShapeDtypeStruct((2, frp, width), f32),
        jax.ShapeDtypeStruct((SMALL, width), f32),
    ]
    pad = V((m + 4 * s, c), bf16)
    full = V((m, c), f32)
    scratch = [
        V((taps, c, c), bf16), V((taps, c, c), bf16), V((m, c), bf16), V((h, c), bf16), V((h, c), bf16), V((m, c), bf16),
        V((SMALL, c), f32), V((n_dp, 8, feats), f32), V((samples, feats), bf16), V((2, n_dp * frp, width), bf16),
        V((2, samples, width), f32), V((2, s, c), f32), V((2, s, c), bf16), V((2, samples, width), bf16), V((2, n_dp * frp, width), bf16),
        V((taps, c, 2 * width), bf16), V((taps, n_hi * rows, 2 * width), bf16), V((taps, n_hi * rows, width), bf16),
        V((n_hi, taps, rows, width), bf16), V((2, n_hi * frp, width), bf16), V((n_hi, 2, frp, width), bf16),
        V((SMALL, c), f32), V((2 + n_hi, SMALL, c), f32),
        pad, pad, V((h, c), bf16), V((h + s, c), bf16),
        full, full, full, full, full, full, full,
        V((h + s, c), bf16), pad, pad, V((m, c), bf16),
        D((3, 8 * n_hi)), D((3, n_dp, n_ch)), D((n_dp,)), D((n_dp,)), D((3, n_ch)), D((3, n_ch)),
        D((2 * n_hi,)), D((n_dp,)), D((n_ch,)), D((n_ch,)),
        D((3, 3)), D((3, 3)), D((3, 2 * n_hi)), D((3, 2 * n_hi)), D((2, n_ch)), D((2, n_ch)), D((n_ch,)), D((n_ch,)),
        D((2 * n_hi,)), D((2 * n_hi,)), D((2 + n_hi,)), D((2 + n_hi,)), D((4,)),
    ]
    return pl.pallas_call(
        partial(step_kernel, n_dp, n_ch),
        out_shape=out,
        in_specs=[hbm, hbm] + [vm] * 8,
        out_specs=[hbm, hbm, vm, vm, vm],
        scratch_shapes=scratch,
        compiler_params=pltpu.CompilerParams(vmem_limit_bytes=63 << 20, collective_id=0, has_side_effects=True),
        name="block_step",
    )(inputs, cot, cond, lens_all, one_w, two_w, res_w, down_w, film_w, small_w)


beta_one = 0.9
beta_two = 0.999
adam_eps = 1e-08
weight_decay = 0.01
rate_large = 0.05
rate_small = 0.3
adam_step = 10


def adam_update(weight, gradient, old_first, old_second, learn_rate, decay_term):
    first_new = beta_one * old_first + (1.0 - beta_one) * gradient
    second_new = beta_two * old_second + (1.0 - beta_two) * gradient * gradient
    step_size = (
        first_new
        / (1.0 - beta_one**adam_step)
        / (jnp.sqrt(second_new / (1.0 - beta_two**adam_step)) + adam_eps)
    )
    return (first_new, second_new, weight - learn_rate * (step_size + decay_term * weight))


def update_kernel(gw, gf, gs, *refs):
    ins, outs = refs[: len(refs) // 2], refs[len(refs) // 2 :]

    def put(i, index, grad, rate, decay):
        w, m, v = (ins[3 * i + j][index] for j in range(3))
        m, v, w = adam_update(w, grad, m, v, rate, decay)
        for j, value in enumerate((m, v, w)):
            outs[3 * i + j][index] = value

    everything = slice(None)
    for k in range(TAPS):
        put(0, (everything, k), gw[k], rate_large, weight_decay)
        put(1, (everything, k), gw[TAPS + 1 + k], rate_large, weight_decay)
    put(2, ..., gw[TAPS], rate_large, weight_decay)
    for k in range(DOWN):
        put(3, (everything, k), gw[2 * TAPS + 1 + k], rate_large, weight_decay)
    frows = ins[12].shape[0]
    for k in range(2):
        put(4, (everything, k), gf[k, pl.ds(0, frows), :], rate_large, weight_decay)
    put(5, ..., gs[pl.ds(0, ins[15].shape[0]), :], rate_small, 0.0)


def update(gw, gf, gs, *state):
    vm = pl.BlockSpec(memory_space=pltpu.VMEM)
    return pl.pallas_call(
        update_kernel,
        out_shape=[jax.ShapeDtypeStruct(a.shape, f32) for a in state],
        in_specs=[vm] * (3 + len(state)),
        out_specs=[vm] * len(state),
        compiler_params=pltpu.CompilerParams(vmem_limit_bytes=32 << 20),
        name="update",
    )(gw, gf, gs, *state)


def body(
    inputs, condition, lengths, cotangent,
    conv1_w, conv1_m, conv1_v, conv2_w, conv2_m, conv2_v, res_w, res_m, res_v,
    down_w, down_m, down_v, film_w, film_m, film_v, small_w, small_m, small_v,
):
    n_dp, n_ch = lax.axis_size("dp"), lax.axis_size("chan")
    lens_all = jnp.broadcast_to(lengths[:, None], (lengths.shape[0], 128))
    cond, film_rows = condition, film_w
    frows = film_w.shape[0]
    if frows % 16:
        short = -frows % 16
        film_rows = jnp.pad(film_w, ((0, short), (0, 0), (0, 0)))
        cond = jnp.pad(condition.reshape(-1, n_dp, frows), ((0, 0), (0, 0), (0, short))).reshape(condition.shape[0], -1)
    output, input_grad, gw, gf, gs = block_step(
        n_dp, n_ch, inputs, cotangent, cond, lens_all, conv1_w, conv2_w, res_w, down_w, film_rows, small_w
    )
    state = update(
        gw, gf, gs,
        conv1_w, conv1_m, conv1_v, conv2_w, conv2_m, conv2_v, res_w, res_m, res_v,
        down_w, down_m, down_v, film_w, film_m, film_v, small_w, small_m, small_v,
    )
    return (output, input_grad, *state)


def solution(mesh):
    in_specs = (
        P("dp", "chan"),
        P("dp", None),
        P("dp"),
        P("dp", "chan"),
        P("dp", None, "chan"),
        P("dp", None, "chan"),
        P("dp", None, "chan"),
        P("dp", None, "chan"),
        P("dp", None, "chan"),
        P("dp", None, "chan"),
        P("dp", "chan"),
        P("dp", "chan"),
        P("dp", "chan"),
        P("dp", None, "chan"),
        P("dp", None, "chan"),
        P("dp", None, "chan"),
        P("dp", None, "chan"),
        P("dp", None, "chan"),
        P("dp", None, "chan"),
        P(None, "chan"),
        P(None, "chan"),
        P(None, "chan"),
    )
    out_specs = (
        P("dp", "chan"),
        P("dp", "chan"),
        P("dp", None, "chan"),
        P("dp", None, "chan"),
        P("dp", None, "chan"),
        P("dp", None, "chan"),
        P("dp", None, "chan"),
        P("dp", None, "chan"),
        P("dp", "chan"),
        P("dp", "chan"),
        P("dp", "chan"),
        P("dp", None, "chan"),
        P("dp", None, "chan"),
        P("dp", None, "chan"),
        P("dp", None, "chan"),
        P("dp", None, "chan"),
        P("dp", None, "chan"),
        P(None, "chan"),
        P(None, "chan"),
        P(None, "chan"),
    )
    return jax.shard_map(body, mesh=mesh, in_specs=in_specs, out_specs=out_specs, check_vma=False)
```

time: 606 us -> 203 us (0.33)
  the two profiles are of different devices: /device:TPU:8 before, /device:TPU:0 now
where the time goes in v1:
time: 203 us; the launch traced here: 202 us
  Pallas kernels  169 us (83%)
  local copies, waits for them, and re-layouts  32.3 us (16%)
    pallas_call x1, Pallas kernels, block_step(): pl.pallas_call(partial(step_kernel, n_dp, n_ch), out_shape=out, in_specs=...  165 us
    unnamed x74, local copies, waits for them, and re-layouts  30.8 us

profile of v1, /device:TPU:0, one launch (start us, length us, event | category | flops | bytes accessed | tf_op | source)
XLA Modules:
  0.0 202.0 jit_solution(7889395952397766481)
XLA Ops:
  0.7 1.7 copy.44.down_w.refs_9_
  2.4 1.5 broadcast_in_dim.2.lens_all
  3.8 1.6 copy.52.refs_10_
  5.5 1.7 copy.53.refs_11_
  7.1 1.7 copy.42.one_w.refs_0_
  8.8 0.8 copy.43.two_w.refs_3_
  9.8 0.8 copy.47.refs_2_
  10.6 0.8 copy.49.refs_4_
  11.4 0.8 copy.50.refs_5_
  12.2 165.4 %block_step.1 = (bf16[2048,128]{1,0:T(8,128)(2,1)}, bf16[4096,128]{1,0:T(8,128)(2,1)}, f32[14,64,128]{2,1,0:T(8,128)}, f32[2,144,128]{2,1,0:T(8,128)}, f32[16,128]{1,0:T(8,128)}) custom-call(bf16[4096,128]{1,0:T(8,128)(2,1)} %inputs.1, bf16[2048,128]{1,0:T(8,128)(2,1)} %cot.1, f32[256,1152]{1,0:T(8,128)} %cond.1, s32[256,128]{1,0:T(8,128)} %broadcast_in_dim.2.lens_all, ...), custom_call_target="tpu_custom_call" | custom-call | tf_op jit(solution)/shard_map/block_step/pallas_call | solution.py:793
  177.7 0.9 copy-done.3
  178.7 0.9 copy-done.4
  179.6 0.9 copy-done.5
  180.6 0.9 copy-done.6
  181.5 0.9 copy-done.7
  182.4 0.9 copy-done.8
  183.3 1.0 copy-done.9
  184.3 0.9 copy-done.10
  185.2 0.9 copy-done.11
  186.1 0.9 copy-done.12
  187.0 0.8 copy-done.15
  190.6 3.5 %update.1 = (f32[64,5,128]{2,1,0:T(8,128)S(1)}, f32[64,5,128]{2,1,0:T(8,128)S(1)}, f32[64,5,128]{2,1,0:T(8,128)S(1)}, f32[64,5,128]{2,1,0:T(8,128)S(1)}, f32[64,...) custom-call(f32[14,64,128]{2,1,0:T(8,128)S(1)} %copy-done.9, ...), custom_call_target="tpu_custom_call" | custom-call | tf_op jit(solution)/shard_map/update/pallas_call | solution.py:848
  200.2 0.8 copy.65
  201.0 1.0 copy.66
  (53 shorter events, 9.1 us)
Async XLA Ops:
  0.7 8.2 %copy-start.22 = (f32[64,5,128]{2,0,1:T(8,128)S(1)}, f32[64,5,128]{2,0,1:T(8,128)}, u32[]{:S(2)}) copy-start(f32[64,5,128]{2,0,1:T(8,128)} %param.29) | copy-start | bytes 491524
  0.7 9.1 %copy-start.24 = (f32[64,5,128]{2,0,1:T(8,128)S(1)}, f32[64,5,128]{2,0,1:T(8,128)}, u32[]{:S(2)}) copy-start(f32[64,5,128]{2,0,1:T(8,128)} %param.28) | copy-start | bytes 491524
  0.7 9.0 %copy-start.23 = (f32[64,5,128]{2,0,1:T(8,128)S(1)}, f32[64,5,128]{2,0,1:T(8,128)}, u32[]{:S(2)}) copy-start(f32[64,5,128]{2,0,1:T(8,128)} %param.27) | copy-start | bytes 491524
  2.4 8.2 %copy-start.25 = (f32[64,5,128]{2,0,1:T(8,128)S(1)}, f32[64,5,128]{2,0,1:T(8,128)}, u32[]{:S(2)}) copy-start(f32[64,5,128]{2,0,1:T(8,128)} %param.30) | copy-start | bytes 491524
  5.5 5.9 %copy-start.26 = (f32[64,5,128]{2,0,1:T(8,128)S(1)}, f32[64,5,128]{2,0,1:T(8,128)}, u32[]{:S(2)}) copy-start(f32[64,5,128]{2,0,1:T(8,128)} %param.31) | copy-start | bytes 491524
  12.2 165.5 %copy-start = (f32[64,5,128]{2,1,0:T(8,128)S(1)}, f32[64,5,128]{2,1,0:T(8,128)}, u32[]{:S(2)}) copy-start(f32[64,5,128]{2,1,0:T(8,128)} %copy.42.one_w.refs_0_) | copy-start | bytes 491524
  12.2 165.5 %copy-start.1 = (f32[64,5,128]{2,1,0:T(8,128)S(1)}, f32[64,5,128]{2,1,0:T(8,128)}, u32[]{:S(2)}) copy-start(f32[64,5,128]{2,1,0:T(8,128)} %copy.43.two_w.refs_3_) | copy-start | bytes 491524
  12.2 165.5 %copy-start.2 = (f32[64,3,128]{2,1,0:T(4,128)S(1)}, f32[64,3,128]{2,1,0:T(4,128)}, u32[]{:S(2)}) copy-start(f32[64,3,128]{2,1,0:T(4,128)} %copy.44.down_w.refs_9_) | copy-start | bytes 294916
  12.2 165.5 %copy-start.13 = (f32[64,128]{1,0:T(8,128)S(1)}, f32[64,128]{1,0:T(8,128)}, u32[]{:S(2)}) copy-start(f32[64,128]{1,0:T(8,128)} %refs_6_.1) | copy-start | bytes 98308
  12.2 165.5 %copy-start.14 = (f32[64,128]{1,0:T(8,128)S(1)}, f32[64,128]{1,0:T(8,128)}, u32[]{:S(2)}) copy-start(f32[64,128]{1,0:T(8,128)} %refs_7_.1) | copy-start | bytes 98308
  177.7 1.0 copy-start.3
  178.7 0.9 copy-start.4
  179.6 0.9 copy-start.5
  180.6 0.9 copy-start.6
  181.5 0.9 copy-start.7
  182.4 0.9 copy-start.8
  183.3 1.0 copy-start.9
  184.3 0.9 copy-start.10
  185.2 0.9 copy-start.11
  186.1 0.9 copy-start.12
  187.0 0.8 copy-start.15
  187.8 0.7 copy-start.16
  196.0 4.1 %copy-start.21 = (bf16[2048,128]{1,0:T(8,128)(2,1)S(1)}, bf16[2048,128]{1,0:T(8,128)(2,1)}, u32[]{:S(2)}) copy-start(bf16[2048,128]{1,0:T(8,128)(2,1)} %get-tuple-element.106) | copy-start | bytes 1572868
  198.1 2.9 %copy-start.20 = (bf16[4096,128]{1,0:T(8,128)(2,1)S(1)}, bf16[4096,128]{1,0:T(8,128)(2,1)}, u32[]{:S(2)}) copy-start(bf16[4096,128]{1,0:T(8,128)(2,1)} %get-tuple-element.107) | copy-start | bytes 3145732
  (3 other events, 2.1 us)

commit v2 on v1

v2 whole, which is shorter than its diff:
```python
from functools import partial

import jax
import jax.numpy as jnp
from jax import lax
from jax.experimental import pallas as pl
from jax.experimental.pallas import tpu as pltpu
from jax.sharding import PartitionSpec as P

f32, bf16 = jnp.float32, jnp.bfloat16
GROUP = 64
TAPS = 5
DOWN = 3
eps_norm = 1e-05


def dot_nn(a, b):
    return lax.dot_general(a, b, (((1,), (0,)), ((), ())), preferred_element_type=f32)


def dot_nt(a, b):
    return lax.dot_general(a, b, (((1,), (1,)), ((), ())), preferred_element_type=f32)


def dot_tn(a, b):
    return lax.dot_general(a, b, (((0,), (0,)), ((), ())), preferred_element_type=f32)


def mish_pair(v):
    u = jnp.exp(-jnp.abs(v))
    pos = v >= 0
    num = jnp.where(pos, 1.0 + 2.0 * u, u * (u + 2.0))
    q = jnp.where(pos, 2.0 * u * u, 2.0)
    r = 1.0 / (num + q)
    w = num * r
    sig = jnp.where(pos, 1.0, u) / (1.0 + u)
    return v * w, w + v * sig * ((q * r) * ((2.0 * num + q) * r))


def wide(tile, lanes):
    return jnp.concatenate([tile] * (lanes // tile.shape[1]), axis=1)


def grid_turn(outer, inner):
    n = outer * inner
    row = lax.broadcasted_iota(jnp.int32, (n, n), 0)
    col = lax.broadcasted_iota(jnp.int32, (n, n), 1)
    return ((row % outer) * inner + row // outer == col).astype(bf16)


def group_sum(values):
    s, c = values.shape
    row = lax.broadcasted_iota(jnp.int32, (128, 128), 0)
    col = lax.broadcasted_iota(jnp.int32, (128, 128), 1)
    ones = (row // GROUP == col // GROUP).astype(f32)
    tall = jnp.concatenate([values[:, i : i + 128] for i in range(0, c, 128)], axis=0)
    tot = lax.dot_general(tall, ones, (((1,), (0,)), ((), ())), precision=lax.Precision.HIGHEST, preferred_element_type=f32)
    return jnp.concatenate([tot[i * s : (i + 1) * s] for i in range(c // 128)], axis=1)


MESH = pl.DeviceIdType.MESH
W_ONE, W_RES, W_TWO, W_DOWN = 0, TAPS, TAPS + 1, 2 * TAPS + 1
N_TAPS = W_DOWN + DOWN
PARTS = ((W_ONE, TAPS + 1), (W_TWO, TAPS), (W_DOWN, DOWN))
G_DOWN, G_RES, G_TWO_A, G_TWO_B, G_ONE_A, G_ONE_B, G_ONE_C = range(7)
SUMS = (
    (W_DOWN, DOWN, True), (W_RES, 1, False), (W_TWO, 3, False), (W_TWO + 3, 2, True),
    (W_ONE, 2, False), (W_ONE + 2, 2, False), (W_ONE + 4, 1, False),
)
SMALL = 16


def step_kernel(
    n_dp, n_ch,
    inputs, cot, cond_h, lens_h, one_w, two_w, res_w, down_w, film_h, small_h,
    output, input_grad, gfin_h, gffin_h, gsfin_h,
    w_all, gw_all, x_raw, cot_raw, out_raw, ig_raw, small, stats, act, wf_all, film_out, film, gfilm, gfa, gwf,
    gfin, gffin, gsfin, rcb, rxb, ryb, sidebuf, rzb, rfx, rfz, rfs, gsm, gsr, cond, lens_row, lens_all, wraw, film_w, small_w,
    xpad, hpad, be, bo, cbuf, res, xh1, m1, dm1, xh2, dm2, gdn, gc2, gc1, gres,
    ag_send, ag_recv, st_send, st_recv, in_send, in_recv, fw_send, fw_recv, fo_send, fo_recv,
    rs_send, rs_recv, rz_send, rz_recv, out_send, out_recv, gf_send, gf_recv, rf_send, rf_recv, gs_send, gs_recv, loc,
):
    dp, ch = lax.axis_index("dp"), lax.axis_index("chan")
    hi, lo, yy, co = dp // 2, dp % 2, ch // 2, ch % 2
    n_hi = n_dp // 2
    dp_x = hi * 2 + 1 - lo
    ch_y = (1 - yy) * 2 + co
    ch_c = yy * 2 + 1 - co
    m, c = x_raw.shape
    h2 = m // 2
    rows, width = res_w.shape
    frp = film_h.shape[0]
    s = lens_h.shape[1] // n_ch
    frames = m // s
    half = frames // 2
    MC = 256 if m % 256 == 0 else m
    NB = 256

    def at(index, size):
        return pl.ds(pl.multiple_of(index * size, size), size)

    def remote(src, dst, ss, rs, device):
        return pltpu.make_async_remote_copy(
            src_ref=src, dst_ref=dst, send_sem=ss, recv_sem=rs, device_id=device, device_id_type=MESH
        )

    barrier = pltpu.get_barrier_semaphore()

    @pl.loop(1, n_dp)
    def _(i):
        pl.semaphore_signal(barrier, inc=1, device_id=((dp + i) % n_dp, ch), device_id_type=MESH)

    for i in range(1, n_ch):
        pl.semaphore_signal(barrier, inc=1, device_id=(dp, (ch + i) % n_ch), device_id_type=MESH)

    def local(i, src, dst):
        copy = pltpu.make_async_copy(src, dst, loc.at[i])
        copy.start()
        return copy

    own_x = local(0, inputs.at[at(ch, m)], x_raw.at[:, at(ch, width)])
    own_cot = local(1, cot.at[at(ch, h2)], cot_raw.at[:, at(ch, width)])
    staged = [
        local(4, cond_h, cond), local(5, lens_h, lens_row), local(6, small_h, small_w),
        local(7, one_w, wraw.at[pl.ds(W_ONE, TAPS)]), local(8, two_w, wraw.at[pl.ds(W_TWO, TAPS)]),
        local(9, down_w, wraw.at[pl.ds(W_DOWN, DOWN)]), local(10, res_w, wraw.at[W_RES]), local(11, film_h, film_w),
    ]
    pad0 = jnp.zeros((2 * s, c), bf16)
    for ref in (xpad, hpad, gc2, gc1):
        ref[pl.ds(0, 2 * s), :] = pad0
        ref[pl.ds((frames + 2) * s, 2 * s), :] = pad0
    bo[pl.ds(0, s), :] = pad0[:s]
    gdn[pl.ds(half * s, s), :] = pad0[:s]
    for copy in staged:
        copy.wait()
    my_rows, my_cols = at(dp, rows), at(ch, width)

    @pl.loop(0, N_TAPS)
    def _(k):
        w_all[k, my_rows, my_cols] = wraw[k].astype(bf16)

    for i in range(2):
        wf_all[i, at(dp, frp), :] = film_w[:, i, :].astype(bf16)
    n_all = lens_all.shape[0]
    on_line = lax.broadcasted_iota(jnp.int32, (n_all, n_all), 0) == lax.broadcasted_iota(jnp.int32, (n_all, n_all), 1)
    across = jnp.sum(jnp.where(on_line, lens_row[...].astype(f32), 0.0), axis=1, keepdims=True)
    lens_all[...] = jnp.broadcast_to(across, lens_all.shape)
    small[pl.ds(0, small_w.shape[0]), my_cols] = small_w[...]
    small[pl.ds(small_w.shape[0], SMALL - small_w.shape[0]), my_cols] = jnp.zeros((SMALL - small_w.shape[0], width), f32)
    values = cond[...]
    feats = values.shape[1] // 128
    ends = (jnp.max(values, axis=0, keepdims=True), jnp.max(-values, axis=0, keepdims=True))
    for e in range(2):
        for i in range(feats):
            stats[0, pl.ds(e * feats + i, 1), :] = ends[e][:, i * 128 : (i + 1) * 128]
    if stats.shape[1] > 2 * feats:
        stats[0, pl.ds(2 * feats, stats.shape[1] - 2 * feats), :] = jnp.zeros((stats.shape[1] - 2 * feats, 128), f32)
    pl.semaphore_wait(barrier, n_dp - 1 + n_ch - 1)

    far, near = hi // 2, hi % 2
    if n_hi == 4:
        line = (far * 2 + 1 - near, (1 - far) * 2 + far, (1 - far) * 3)
    else:
        line = None

    def along(step, middle=None):
        if line is not None:
            for j, h in enumerate(line):
                step(h)
                if j == 1 and middle is not None:
                    middle()
        else:

            @pl.loop(1, n_hi)
            def _(i):
                step((hi + i) % n_hi)

            if middle is not None:
                middle()

    def block(p, d, q):
        t0, nt = PARTS[p]
        return w_all.at[pl.ds(t0, nt), at(d, rows), at(q, width)]

    def pass_on(p, d, q, slot, device):
        return remote(block(p, d, q), block(p, d, q), ag_send.at[p, slot], ag_recv.at[p, d, q], device)

    def to_y(p, h):
        return pass_on(p, h * 2 + lo, ch, n_hi + h, (dp, ch_y))

    def to_x(p, h, v):
        return pass_on(p, h * 2 + lo, v * 2 + co, 2 * n_hi + 2 * h + v, (dp_x, ch))

    def to_c(p, h, l, v):
        return pass_on(p, h * 2 + l, v * 2 + co, 4 * n_hi + 4 * h + 2 * l + v, (dp, ch_c))

    def to_z(p, h):
        return pass_on(p, dp, ch, h, (h * 2 + lo, ch))

    def landed(p, d, q):
        pass_on(p, d, q, 0, (dp, ch)).wait_recv()

    def ag_far(p):
        along(lambda h: to_z(p, h).start())

    def ag_own(p):
        to_y(p, hi).start()
        to_x(p, hi, yy).start()
        to_c(p, hi, lo, yy).start()

    def from_z(p, h):
        landed(p, h * 2 + lo, ch)
        to_y(p, h).start()
        to_x(p, h, yy).start()
        to_c(p, h, lo, yy).start()

    def from_y(p, h):
        landed(p, h * 2 + lo, ch_y)
        to_x(p, h, 1 - yy).start()
        to_c(p, h, lo, 1 - yy).start()

    def from_x(p, h, v):
        landed(p, h * 2 + 1 - lo, v * 2 + co)
        to_c(p, h, 1 - lo, v).start()

    def ag_z(p, middle=None):
        along(lambda h: from_z(p, h), middle)

    def ag_y(p):
        along(lambda h: from_y(p, h))

    def ag_x(p):
        for v in (yy, 1 - yy):
            from_x(p, hi, v)
            along(lambda h: from_x(p, h, v))

    def ag_core(p):
        @pl.loop(0, n_dp)
        def _(d):
            for v in range(n_ch // 2):
                landed(p, d, v * 2 + 1 - co)

    def ag_done(p):
        along(lambda h: to_z(p, h).wait_send())

        @pl.loop(0, n_hi)
        def _(h):
            to_y(p, h).wait_send()
            for v in range(2):
                to_x(p, h, v).wait_send()
                for l in range(2):
                    to_c(p, h, l, v).wait_send()

    def swap_in(src, dst, n, k, i):
        q = (ch + i) % n_ch
        return remote(src.at[at(q, n)], dst.at[:, my_cols], in_send.at[k, i], in_recv.at[k, i], (dp, q))

    def swap_in_wait(src, dst, n, k):
        for i in range(1, n_ch):
            q = (ch + n_ch - i) % n_ch
            remote(src.at[at(q, n)], dst.at[:, at(q, width)], in_send.at[k, i], in_recv.at[k, i], (dp, q)).wait_recv()
        for i in range(1, n_ch):
            swap_in(src, dst, n, k, i).wait_send()

    def swap_out(src, dst, n, k, i):
        q = (ch + i) % n_ch
        return remote(src.at[:, at(q, width)], dst.at[at(ch, n)], out_send.at[k, i], out_recv.at[k, i], (dp, q))

    def swap_out_wait(src, dst, n, k):
        for i in range(1, n_ch):
            q = (ch + n_ch - i) % n_ch
            remote(src.at[:, at(q, width)], dst.at[at(q, n)], out_send.at[k, i], out_recv.at[k, i], (dp, q)).wait_recv()
        for i in range(1, n_ch):
            swap_out(src, dst, n, k, i).wait_send()

    def small_swap(i, q):
        return remote(small.at[:, at(q, width)], small.at[:, at(q, width)], in_send.at[2, i], in_recv.at[2, i], (dp, (ch + i) % n_ch))

    def bounds_x():
        return remote(stats.at[0], stats.at[1], st_send.at[n_hi], st_recv.at[n_hi], (dp_x, ch))

    def bounds_z(h):
        return remote(stats.at[2], stats.at[3 + hi], st_send.at[h], st_recv.at[hi], (h * 2 + lo, ch))

    def bounds_in(h):
        return remote(stats.at[2], stats.at[3 + h], st_send.at[h], st_recv.at[h], (h * 2 + lo, ch))

    def film_block(d):
        return wf_all.at[:, at(d, frp), :]

    def film_pass(d, slot, device):
        return remote(film_block(d), film_block(d), fw_send.at[slot], fw_recv.at[d], device)

    def film_x():
        return film_pass(dp, 0, (dp_x, ch))

    def film_z(i, l):
        return film_pass(hi * 2 + l, 2 * i + l, ((hi + i) % n_hi * 2 + lo, ch))

    def film_swap(i, q):
        return remote(
            film_out.at[:, at(q, s), :], film.at[:, :, my_cols], fo_send.at[i], fo_recv.at[i], (dp, q)
        )

    bounds_x().start()
    film_x().start()
    ag_far(0)
    ag_own(0)
    ag_own(1)
    for i in range(1, n_ch):
        small_swap(i, ch).start()
    bounds_x().wait_recv()
    stats[2] = jnp.maximum(stats[0], stats[1])
    stats[3 + hi] = stats[2]
    along(lambda h: bounds_z(h).start())
    from_y(0, hi)
    ag_z(0, lambda: ag_far(1))
    for i in range(1, n_ch):
        swap_in(inputs, x_raw, m, 0, i).start()
    from_y(1, hi)
    ag_y(0)
    along(lambda h: bounds_in(h).wait_recv())
    best = stats[3]
    for h in range(1, n_hi):
        best = jnp.maximum(best, stats[3 + h])
    low = -jnp.concatenate([best[feats + i : feats + i + 1, :] for i in range(feats)], axis=1)
    span = jnp.concatenate([best[i : i + 1, :] for i in range(feats)], axis=1) - low
    slope = 2.0 / jnp.maximum(span, 1.0)
    CB = 64

    @pl.loop(0, cond.shape[0] // CB)
    def _(i):
        v = (cond[at(i, CB), :] - low) * slope - 1.0
        act[at(i, CB), :] = mish_pair(v)[0].astype(bf16)

    def film_on():
        film_pass(dp_x, 0, (dp, ch)).wait_recv()

        @pl.loop(1, n_hi)
        def _(i):
            for l in range(2):
                film_z(i, l).start()

    ag_z(1, film_on)
    ag_far(2)
    ag_x(0)

    lens_ref = lens_all.at[at(ch, s)]

    def mask(t):
        return wide((lens_ref[...] > t).astype(f32), c)

    count = wide(lens_ref[...].astype(f32), c) * GROUP
    own_x.wait()
    swap_in_wait(inputs, x_raw, m, 0)
    sb = 256 // frames
    turn = grid_turn(sb, frames)
    for b in range(s // sb):
        y = dot_nn(turn, x_raw[pl.ds(b * 256, 256), :])
        lens_b = lens_ref[pl.ds(b * sb, sb), :]
        for t in range(frames):
            keep = wide((lens_b > t).astype(f32), c)
            xpad[pl.ds((t + 2) * s + b * sb, sb), :] = (y[t * sb : (t + 1) * sb] * keep).astype(bf16)

    def conv_fwd(src, base, store):
        @pl.loop(0, c // NB)
        def _(n):
            cols = at(n, NB)
            for mi in range(m // MC):
                acc = dot_nn(src[pl.ds(mi * MC, MC), :], w_all[base, :, cols])
                for k in range(1, TAPS):
                    acc += dot_nn(src[pl.ds(mi * MC + k * s, MC), :], w_all[base + k, :, cols])
                store(pl.ds(mi * MC, MC), cols, acc)

    def conv_bwd(src, base, store):
        @pl.loop(0, c // NB)
        def _(n):
            cols = at(n, NB)
            for mi in range(m // MC):
                acc = dot_nt(src[pl.ds(mi * MC + (TAPS - 1) * s, MC), :], w_all[base, cols, :])
                for k in range(1, TAPS):
                    acc += dot_nt(src[pl.ds(mi * MC + (TAPS - 1 - k) * s, MC), :], w_all[base + k, cols, :])
                store(pl.ds(mi * MC, MC), cols, acc)

    def conv_grad(src, g, base, first, last):
        @pl.loop(first, last)
        def _(k):
            shifted = pl.ds(pl.multiple_of((TAPS - 1 - k) * s, s), m)
            for n in range(c // NB):
                cols = pl.ds(n * NB, NB)
                gw_all[base + k, :, cols] = dot_tn(src[pl.ds(2 * s, m), :], g[shifted, cols]).astype(bf16)

    def norm_stats(bias):
        tot = jnp.zeros((s, c), f32)
        for t in range(frames):
            tot += (cbuf[pl.ds(t * s, s), :] + bias) * mask(t)
        mean = group_sum(tot) / count
        tot = jnp.zeros((s, c), f32)
        for t in range(frames):
            d = (cbuf[pl.ds(t * s, s), :] + bias - mean) * mask(t)
            tot += d * d
        return mean, lax.rsqrt(group_sum(tot) / count + eps_norm)

    def row(i):
        return small[pl.ds(i, 1), :]

    def keep_c(part, cols, acc):
        cbuf[part, cols] = acc

    ag_core(0)
    ag_y(1)
    ag_own(2)
    conv_fwd(xpad, W_ONE, keep_c)
    for i in range(1, n_ch):
        small_swap(i, (ch + n_ch - i) % n_ch).wait_recv()
    bias = row(0)
    @pl.loop(1, n_hi)
    def _(i):
        for l in range(2):
            film_pass((hi + i) % n_hi * 2 + l, 0, (dp, ch)).wait_recv()

    for i in range(2):
        film_out[i] = dot_nn(act[...], wf_all[i]) + small[pl.ds(6 + i, 1), my_cols]
    for i in range(1, n_ch):
        film_swap(i, (ch + i) % n_ch).start()
    for i in range(2):
        film[i, :, my_cols] = film_out[i, at(ch, s), :]

    for n in range(c // NB):
        cols = pl.ds(n * NB, NB)
        for mi in range(m // MC):
            res[pl.ds(mi * MC, MC), cols] = dot_nn(xpad[pl.ds(2 * s + mi * MC, MC), :], w_all[W_RES, :, cols])
    mean, rstd1 = norm_stats(bias)
    ag_z(2)
    ag_x(1)
    for i in range(1, n_ch):
        swap_in(cot, cot_raw, h2, 1, i).start()
    for i in range(1, n_ch):
        q = (ch + n_ch - i) % n_ch
        remote(film_out.at[:, at(q, s), :], film.at[:, :, at(q, width)], fo_send.at[i], fo_recv.at[i], (dp, q)).wait_recv()
    for t in range(frames):
        part = pl.ds(t * s, s)
        xh = (cbuf[part, :] + bias - mean) * rstd1
        mi, dmi = mish_pair(xh * row(1) + row(2))
        xh1[part, :] = xh
        m1[part, :] = mi
        dm1[part, :] = dmi
        hpad[pl.ds((t + 2) * s, s), :] = ((film[0] * mi + film[1]) * mask(t)).astype(bf16)
    from_y(2, hi)
    ag_y(2)
    ag_core(1)
    conv_fwd(hpad, W_TWO, keep_c)
    bias = row(3)
    mean, rstd2 = norm_stats(bias)
    for t in range(frames):
        part = pl.ds(t * s, s)
        xh = (cbuf[part, :] + bias - mean) * rstd2
        mi, dmi = mish_pair(xh * row(4) + row(5))
        xh2[part, :] = xh
        dm2[part, :] = dmi
        val = ((mi + res[part, :] + row(8)) * mask(t)).astype(bf16)
        if t % 2 == 0:
            be[pl.ds(t // 2 * s, s), :] = val
        else:
            bo[pl.ds((t // 2 + 1) * s, s), :] = val
    sh = 256 // half
    turn_h = grid_turn(sh, half)
    hm = half * s
    back_h = grid_turn(half, sh)
    dbase = W_DOWN
    obuf = res.at[pl.ds(0, hm)]
    taps_in = (bo, be, bo)
    taps_at = (0, 0, s)
    ag_x(2)
    own_cot.wait()
    swap_in_wait(cot, cot_raw, h2, 1)
    for b in range(s // sh):
        y = dot_nn(turn_h, cot_raw[pl.ds(b * 256, 256), :])
        lens_b = lens_ref[pl.ds(b * sh, sh), :]
        for j in range(half):
            keep = wide((lens_b > 2 * j).astype(f32), c)
            gdn[pl.ds(j * s + b * sh, sh), :] = (y[j * sh : (j + 1) * sh] * keep).astype(bf16)

    results = []

    def side(p):
        return sum(nt for _, nt, y_first in SUMS[:p] if y_first)

    def rs_core(p, v):
        t0, nt, y_first = SUMS[p]
        return remote(
            gw_all.at[pl.ds(t0, nt), :, at(v * 2 + 1 - co, width)],
            rcb.at[pl.ds(t0, nt), :, pl.ds(v * width, width)],
            rs_send.at[p, v], rs_recv.at[p, v], (dp, ch_c),
        )

    def rs_x(p, h):
        t0, nt, y_first = SUMS[p]
        src = sidebuf if y_first else rcb
        dst = ryb if y_first else rxb
        t1 = side(p) if y_first else t0
        return remote(
            src.at[pl.ds(t1, nt), at(h * 2 + 1 - lo, rows), :],
            dst.at[pl.ds(t0, nt), at(h, rows), :],
            rz_send.at[p, n_hi + h], rz_recv.at[p, n_hi + h], (dp_x, ch),
        )

    def rs_y(p):
        t0, nt, y_first = SUMS[p]
        src = rcb if y_first else rxb
        dst = sidebuf.at[pl.ds(side(p), nt)] if y_first else ryb.at[pl.ds(t0, nt)]
        return remote(src.at[pl.ds(t0, nt), :, at(1 - yy, width)], dst, rs_send.at[p, 2], rs_recv.at[p, 2], (dp, ch_y))

    def rs_z(p, i):
        t0, nt, y_first = SUMS[p]
        h = (hi + i) % n_hi
        return remote(
            ryb.at[pl.ds(t0, nt), at(h, rows), :], rzb.at[i, pl.ds(t0, nt)], rz_send.at[p, i], rz_recv.at[p, i], (h * 2 + lo, ch)
        )

    def rs_start(p):
        for v in range(2):
            rs_core(p, v).start()

    def plus(a, b):
        return (a.astype(f32) + b.astype(f32)).astype(bf16)

    def rs_x_start(p):
        @pl.loop(0, n_hi)
        def _(h):
            rs_x(p, h).start()

    def rs_z_start(p):
        @pl.loop(1, n_hi)
        def _(i):
            rs_z(p, i).start()

    def rs_after_core(p):
        for v in range(2):
            rs_core(p, v).wait()

        @pl.loop(SUMS[p][0], SUMS[p][0] + SUMS[p][1])
        def _(k):
            for v in range(2):
                cols = pl.ds(v * width, width)
                rcb[k, :, cols] = plus(rcb[k, :, cols], gw_all[k, :, at(v * 2 + co, width)])

        if SUMS[p][2]:
            rs_y(p).start()
        else:
            rs_x_start(p)

    def rs_after_x(p):
        t0 = SUMS[p][0]

        @pl.loop(0, n_hi)
        def _(h):
            rs_x(p, h).wait()

        @pl.loop(SUMS[p][0], SUMS[p][0] + SUMS[p][1])
        def _(k):
            for h in range(n_hi):
                part = pl.ds(h * rows, rows)
                if SUMS[p][2]:
                    ryb[k, part, :] = plus(ryb[k, part, :], sidebuf[k - t0 + side(p), at(h * 2 + lo, rows), :])
                else:
                    rxb[k, part, :] = plus(rxb[k, part, :], rcb[k, at(h * 2 + lo, rows), :])

        if SUMS[p][2]:
            rs_z_start(p)
        else:
            rs_y(p).start()

    def rs_after_y(p):
        t0 = SUMS[p][0]

        rs_y(p).wait()

        @pl.loop(SUMS[p][0], SUMS[p][0] + SUMS[p][1])
        def _(k):
            if SUMS[p][2]:
                sidebuf[k - t0 + side(p)] = plus(sidebuf[k - t0 + side(p)], rcb[k, :, at(yy, width)])
            else:
                ryb[k] = plus(ryb[k], rxb[k, :, at(yy, width)])

        if SUMS[p][2]:
            rs_x_start(p)
        else:
            rs_z_start(p)

    def rs_after_z(p):
        t0, nt, y_first = SUMS[p]

        @pl.loop(1, n_hi)
        def _(i):
            rs_z(p, i).wait()

        @pl.loop(t0, t0 + nt)
        def _(k):
            def more(i, tot):
                return tot + rzb[i, k].astype(f32)

            gfin[k] = lax.fori_loop(1, n_hi, more, ryb[k, at(hi, rows), :].astype(f32))

        results.append(local(12 + p, gfin.at[pl.ds(t0, nt)], gfin_h.at[pl.ds(t0, nt)]))

    for k in range(DOWN):
        for n in range(c // NB):
            cols = pl.ds(n * NB, NB)
            gw_all[dbase + k, :, cols] = dot_tn(taps_in[k][pl.ds(taps_at[k], hm), :], gdn[pl.ds(0, hm), cols]).astype(bf16)
    rs_start(G_DOWN)
    ag_core(2)
    for n in range(c // NB):
        cols = pl.ds(n * NB, NB)
        acc = dot_nn(bo[pl.ds(0, hm), :], w_all[dbase, :, cols])
        acc += dot_nn(be[...], w_all[dbase + 1, :, cols])
        acc += dot_nn(bo[pl.ds(s, hm), :], w_all[dbase + 2, :, cols])
        obuf[:, cols] = acc
    for b in range(s // sh):
        pieces = []
        lens_b = lens_ref[pl.ds(b * sh, sh), :]
        for j in range(half):
            keep = wide((lens_b > 2 * j).astype(f32), c)
            pieces.append(((obuf[pl.ds(j * s + b * sh, sh), :] + row(9)) * keep).astype(bf16))
        out_raw[pl.ds(b * 256, 256), :] = dot_nn(back_h, jnp.concatenate(pieces, axis=0)).astype(bf16)
    for i in range(1, n_ch):
        swap_out(out_raw, output, h2, 0, i).start()
    own_out = local(2, out_raw.at[:, my_cols], output.at[at(ch, h2)])

    for n in range(c // NB):
        cols = pl.ds(n * NB, NB)
        ge = dot_nt(gdn[pl.ds(0, hm), :], w_all[dbase + 1, cols, :])
        go = dot_nt(gdn[pl.ds(0, hm), :], w_all[dbase + 2, cols, :])
        go += dot_nt(gdn[pl.ds(s, hm), :], w_all[dbase, cols, :])
        for j in range(half):
            cbuf[pl.ds(2 * j * s, s), cols] = ge[j * s : (j + 1) * s]
            cbuf[pl.ds((2 * j + 1) * s, s), cols] = go[j * s : (j + 1) * s]

    rs_after_core(G_DOWN)
    tot = jnp.zeros((s, c), f32)
    for j in range(half):
        tot += gdn[pl.ds(j * s, s), :].astype(f32)
    gs = [None] * SMALL
    gs[9] = jnp.sum(tot, axis=0, keepdims=True)
    tot = jnp.zeros((s, c), f32)
    for t in range(frames):
        part = pl.ds(t * s, s)
        g = cbuf[part, :] * mask(t)
        tot += g
        gres[part, :] = g.astype(bf16)
    gs[8] = jnp.sum(tot, axis=0, keepdims=True)
    for n in range(c // NB):
        cols = pl.ds(n * NB, NB)
        gw_all[W_RES, :, cols] = dot_tn(xpad[pl.ds(2 * s, m), :], gres[:, cols]).astype(bf16)
    rs_start(G_RES)

    def norm_back(xh, dm, gain, rstd, dst, scale):
        a1 = jnp.zeros((s, c), f32)
        a2 = jnp.zeros((s, c), f32)
        for t in range(frames):
            part = pl.ds(t * s, s)
            dy = cbuf[part, :] * mask(t) * dm[part, :]
            if scale is not None:
                dy = dy * scale
            dm[part, :] = dy
            a1 += dy
            a2 += dy * xh[part, :]
        g1 = group_sum(a1 * gain) / count
        g2 = group_sum(a2 * gain) / count
        tot = jnp.zeros((s, c), f32)
        for t in range(frames):
            part = pl.ds(t * s, s)
            dp_t = rstd * (dm[part, :] * gain - mask(t) * (g1 + xh[part, :] * g2))
            tot += dp_t
            dst[pl.ds((t + 2) * s, s), :] = dp_t.astype(bf16)
        return [jnp.sum(v, axis=0, keepdims=True) for v in (tot, a2, a1)]

    gs[3:6] = norm_back(xh2, dm2, row(4), rstd2, gc2, None)
    rs_after_core(G_RES)
    conv_bwd(gc2, W_TWO, keep_c)
    tot1 = jnp.zeros((s, c), f32)
    tot2 = jnp.zeros((s, c), f32)
    for t in range(frames):
        part = pl.ds(t * s, s)
        g = cbuf[part, :] * mask(t)
        tot1 += g * m1[part, :]
        tot2 += g
    gfilm[0] = tot1.astype(bf16)
    gfilm[1] = tot2.astype(bf16)
    gs[6] = jnp.sum(tot1, axis=0, keepdims=True)
    gs[7] = jnp.sum(tot2, axis=0, keepdims=True)

    def film_back(i):
        q = (ch + i) % n_ch
        return remote(gfilm.at[:, :, at(q, width)], gfa.at[:, at(ch, s), :], gf_send.at[i], gf_recv.at[i], (dp, q))

    for i in range(1, n_ch):
        film_back(i).start()
    gfa[:, at(ch, s), :] = gfilm[:, :, my_cols]
    conv_grad(hpad, gc2, W_TWO, 0, 3)
    rs_start(G_TWO_A)
    conv_grad(hpad, gc2, W_TWO, 3, TAPS)
    rs_start(G_TWO_B)
    rs_after_core(G_TWO_A)
    gs[0:3] = norm_back(xh1, dm1, row(1), rstd1, gc1, film[0])
    for i in range(1, n_ch):
        q = (ch + n_ch - i) % n_ch
        remote(gfilm.at[:, :, at(q, width)], gfa.at[:, at(q, s), :], gf_send.at[i], gf_recv.at[i], (dp, q)).wait_recv()
    for i in range(2):
        gwf[i] = dot_tn(act[...], gfa[i]).astype(bf16)

    def rf_z(i):
        h = (hi + i) % n_hi
        return remote(gwf.at[:, at(h, 2 * frp), :], rfz.at[i], rf_send.at[i], rf_recv.at[i], (h * 2 + lo, ch))

    def rf_x():
        return remote(rfs.at[:, at(1 - lo, frp), :], rfx, rf_send.at[0], rf_recv.at[0], (dp_x, ch))

    @pl.loop(1, n_hi)
    def _(i):
        rf_z(i).start()

    rs_after_core(G_TWO_B)
    rs_after_y(G_DOWN)
    rs_after_x(G_RES)
    zero = jnp.zeros((1, c), f32)
    for i in range(SMALL):
        gsm[pl.ds(i, 1), :] = gs[i] if gs[i] is not None else zero

    def small_pass(i, device):
        return remote(gsm, gsr.at[i], gs_send.at[i], gs_recv.at[i], device)

    small_pass(0, (dp, ch_c)).start()
    def keep_ig(part, cols, acc):
        cbuf[part, cols] = acc + dot_nt(gres[part, :], w_all[W_RES, cols, :])

    conv_bwd(gc1, W_ONE, keep_ig)
    back = grid_turn(frames, sb)
    for b in range(s // sb):
        lens_b = lens_ref[pl.ds(b * sb, sb), :]
        pieces = [
            (cbuf[pl.ds(t * s + b * sb, sb), :] * wide((lens_b > t).astype(f32), c)).astype(bf16) for t in range(frames)
        ]
        ig_raw[pl.ds(b * 256, 256), :] = dot_nn(back, jnp.concatenate(pieces, axis=0)).astype(bf16)
    rs_after_x(G_TWO_A)
    for i in range(1, n_ch):
        swap_out(ig_raw, input_grad, m, 1, i).start()
    own_ig = local(3, ig_raw.at[:, my_cols], input_grad.at[at(ch, m)])

    small_pass(0, (dp, ch_c)).wait()
    gsm[...] += gsr[0]
    small_pass(1, (dp_x, ch)).start()
    conv_grad(xpad, gc1, W_ONE, 0, 2)
    rs_start(G_ONE_A)
    rs_after_y(G_TWO_B)
    conv_grad(xpad, gc1, W_ONE, 2, 4)
    rs_start(G_ONE_B)
    rs_after_core(G_ONE_A)
    rs_after_x(G_DOWN)
    conv_grad(xpad, gc1, W_ONE, 4, 5)
    rs_start(G_ONE_C)
    rs_after_core(G_ONE_B)
    rs_after_y(G_RES)
    rs_after_core(G_ONE_C)
    small_pass(1, (dp_x, ch)).wait()
    gsm[...] += gsr[1]
    small_pass(2, (dp, ch_y)).start()
    rs_after_y(G_TWO_A)
    rs_after_x(G_TWO_B)
    @pl.loop(1, n_hi)
    def _(i):
        rf_z(i).wait()

    for v in range(2):
        def more(i, tot):
            return tot + rfz[i, v].astype(f32)

        rfs[v] = lax.fori_loop(1, n_hi, more, gwf[v, at(hi, 2 * frp), :].astype(f32)).astype(bf16)
    rf_x().start()
    for p in range(3):
        ag_done(p)
    bounds_x().wait_send()
    along(lambda h: bounds_z(h).wait_send())

    @pl.loop(1, n_hi)
    def _(i):
        for l in range(2):
            film_z(i, l).wait_send()

    film_x().wait_send()
    for i in range(1, n_ch):
        small_swap(i, ch).wait_send()
        film_swap(i, (ch + i) % n_ch).wait_send()
        film_back(i).wait_send()
    rs_after_z(G_RES)
    rs_after_z(G_DOWN)
    rs_after_x(G_ONE_A)
    rs_after_z(G_TWO_B)
    rs_after_x(G_ONE_B)
    small_pass(2, (dp, ch_y)).wait()
    gsm[...] += gsr[2]

    def small_z(i):
        return small_pass(2 + i, ((hi + i) % n_hi * 2 + lo, ch))

    @pl.loop(1, n_hi)
    def _(i):
        small_z(i).start()

    rs_after_y(G_ONE_A)
    rs_after_x(G_ONE_C)
    rs_after_z(G_TWO_A)
    rf_x().wait()
    for v in range(2):
        gffin[v] = rfs[v, at(lo, frp), :].astype(f32) + rfx[v].astype(f32)
    results.append(local(12 + len(SUMS), gffin, gffin_h))

    rs_after_y(G_ONE_B)
    rs_after_y(G_ONE_C)
    rs_after_z(G_ONE_A)
    @pl.loop(1, n_hi)
    def _(i):
        small_z(i).wait()

    def more_small(i, tot):
        return tot + gsr[2 + i, :, my_cols]

    gsfin[...] = lax.fori_loop(1, n_hi, more_small, gsm[:, my_cols])
    results.append(local(13 + len(SUMS), gsfin, gsfin_h))
    rs_after_z(G_ONE_B)
    rs_after_z(G_ONE_C)

    for copy in results:
        copy.wait()
    own_out.wait()
    own_ig.wait()
    swap_out_wait(out_raw, output, h2, 0)
    swap_out_wait(ig_raw, input_grad, m, 1)


def block_step(n_dp, n_ch, inputs, cot, cond, lens, one_w, two_w, res_w, down_w, film_w, small_w):
    rows, width = res_w.shape
    c = rows * n_dp
    samples = lens.shape[1]
    s = samples // n_ch
    m = inputs.shape[0] // n_ch
    h = m // 2
    frp = film_w.shape[0]
    feats = cond.shape[1]
    n_hi = n_dp // 2
    taps = N_TAPS
    V = pltpu.VMEM
    D = pltpu.SemaphoreType.DMA
    hbm = pl.BlockSpec(memory_space=pl.ANY)
    out = [
        jax.ShapeDtypeStruct((h * n_ch, width), bf16),
        jax.ShapeDtypeStruct((m * n_ch, width), bf16),
        jax.ShapeDtypeStruct((taps, rows, width), f32),
        jax.ShapeDtypeStruct((2, frp, width), f32),
        jax.ShapeDtypeStruct((SMALL, width), f32),
    ]
    pad = V((m + 4 * s, c), bf16)
    full = V((m, c), f32)
    scratch = [
        V((taps, c, c), bf16), V((taps, c, c), bf16), V((m, c), bf16), V((h, c), bf16), V((h, c), bf16), V((m, c), bf16),
        V((SMALL, c), f32), V((3 + n_hi, -(-feats // 512) * 8, 128), f32), V((samples, feats), bf16), V((2, n_dp * frp, width), bf16),
        V((2, samples, width), f32), V((2, s, c), f32), V((2, s, c), bf16), V((2, samples, width), bf16), V((2, n_dp * frp, width), bf16),
        *[V(o.shape, o.dtype) for o in out[2:]],
        V((taps, c, 2 * width), bf16), V((taps, n_hi * rows, 2 * width), bf16), V((taps, n_hi * rows, width), bf16), V((sum(nt for _, nt, y_first in SUMS if y_first), c, width), bf16),
        V((n_hi, taps, rows, width), bf16), V((2, frp, width), bf16), V((n_hi, 2, 2 * frp, width), bf16), V((2, 2 * frp, width), bf16),
        V((SMALL, c), f32), V((2 + n_hi, SMALL, c), f32),
        V((samples, feats), f32), V((1, samples), jnp.int32), V((samples, 128), f32), V((taps, rows, width), f32), V(film_w.shape, f32), V(small_w.shape, f32),
        pad, pad, V((h, c), bf16), V((h + s, c), bf16),
        full, full, full, full, full, full, full,
        V((h + s, c), bf16), pad, pad, V((m, c), bf16),
        D((3, 8 * n_hi)), D((3, n_dp, n_ch)), D((n_hi + 1,)), D((n_hi + 1,)), D((3, n_ch)), D((3, n_ch)),
        D((2 * n_hi,)), D((n_dp,)), D((n_ch,)), D((n_ch,)),
        D((len(SUMS), 3)), D((len(SUMS), 3)), D((len(SUMS), 2 * n_hi)), D((len(SUMS), 2 * n_hi)), D((2, n_ch)), D((2, n_ch)), D((n_ch,)), D((n_ch,)),
        D((n_hi,)), D((n_hi,)), D((2 + n_hi,)), D((2 + n_hi,)), D((14 + len(SUMS),)),
    ]
    return pl.pallas_call(
        partial(step_kernel, n_dp, n_ch),
        out_shape=out,
        in_specs=[hbm] * 10,
        out_specs=[hbm] * 5,
        scratch_shapes=scratch,
        compiler_params=pltpu.CompilerParams(vmem_limit_bytes=63 << 20, collective_id=0, has_side_effects=True),
        name="block_step",
    )(inputs, cot, cond, lens, one_w, two_w, res_w, down_w, film_w, small_w)


beta_one = 0.9
beta_two = 0.999
adam_eps = 1e-08
weight_decay = 0.01
rate_large = 0.05
rate_small = 0.3
adam_step = 10


def adam_update(weight, gradient, old_first, old_second, learn_rate, decay_term):
    first_new = beta_one * old_first + (1.0 - beta_one) * gradient
    second_new = beta_two * old_second + (1.0 - beta_two) * gradient * gradient
    step_size = (
        first_new
        / (1.0 - beta_one**adam_step)
        / (jnp.sqrt(second_new / (1.0 - beta_two**adam_step)) + adam_eps)
    )
    return (first_new, second_new, weight - learn_rate * (step_size + decay_term * weight))


def update_kernel(n, a_in, b_in, *refs):
    ins, a_out, b_out, refs = refs[:n], refs[n], refs[n + 1], refs[n + 2 :]
    outs, bufs, results, refs = refs[: n - 3], refs[n - 3 : 2 * n - 3], refs[2 * n - 3 : 3 * n - 6], refs[3 * n - 6 :]
    a_buf, b_buf, sem_in, sem_out, sem_ab = refs
    order = (2, 4, 5, 3, 1, 0)
    loads = [pltpu.make_async_copy(ins[i], bufs[i], sem_in.at[i]) for i in range(n)]
    stores = [pltpu.make_async_copy(results[i], outs[i], sem_out.at[i]) for i in range(n - 3)]
    gw, gf, gs = bufs[:3]
    big = [pltpu.make_async_copy(src, dst, sem_ab.at[i]) for i, (src, dst) in enumerate(((a_in, a_buf), (b_in, b_buf), (a_buf, a_out), (b_buf, b_out)))]
    for copy in loads[:3]:
        copy.start()
    for i in order:
        for j in range(3):
            loads[3 + 3 * i + j].start()
    big[0].start()
    big[1].start()

    def put(i, index, grad, rate, decay):
        w, m, v = (bufs[3 + 3 * i + j][index] for j in range(3))
        for j, value in enumerate(adam_update(w, grad, m, v, rate, decay)):
            results[3 * i + j][index] = value

    for copy in loads[:3]:
        copy.wait()
    frows = ins[3 + 12].shape[0]
    for i in order:
        for j in range(3):
            loads[3 + 3 * i + j].wait()
        if i in (0, 1, 3):
            base, taps = ((W_ONE, TAPS), (W_TWO, TAPS), None, (W_DOWN, DOWN))[i]
            for k in range(taps):
                put(i, k, gw[base + k], rate_large, weight_decay)
        elif i == 2:
            put(i, ..., gw[W_RES], rate_large, weight_decay)
        elif i == 4:
            for k in range(2):
                put(i, (slice(None), k), gf[k, pl.ds(0, frows), :], rate_large, weight_decay)
        else:
            put(i, ..., gs[pl.ds(0, ins[3 + 15].shape[0]), :], rate_small, 0.0)
        for j in range(3):
            stores[3 * i + j].start()
    for i in range(2):
        big[i].wait()
        big[2 + i].start()
    for copy in stores:
        copy.wait()
    big[2].wait()
    big[3].wait()


def update(output, input_grad, gw, gf, gs, *state):
    hbm = pl.BlockSpec(memory_space=pl.ANY)
    acts = (output, input_grad)
    arrays = (gw, gf, gs, *state)
    n = len(arrays)
    bufs = [pltpu.VMEM(a.shape, f32) for a in arrays]
    return pl.pallas_call(
        partial(update_kernel, n),
        out_shape=[jax.ShapeDtypeStruct(a.shape, a.dtype) for a in (*acts, *state)],
        in_specs=[hbm] * (n + 2),
        out_specs=[hbm] * (len(state) + 2),
        scratch_shapes=[
            *bufs, *bufs[3:], *[pltpu.VMEM(a.shape, a.dtype) for a in acts],
            pltpu.SemaphoreType.DMA((n,)), pltpu.SemaphoreType.DMA((n,)), pltpu.SemaphoreType.DMA((4,)),
        ],
        compiler_params=pltpu.CompilerParams(vmem_limit_bytes=60 << 20),
        name="update",
    )(*acts, *arrays)


def body(
    inputs, condition, lengths, cotangent,
    conv1_w, conv1_m, conv1_v, conv2_w, conv2_m, conv2_v, res_w, res_m, res_v,
    down_w, down_m, down_v, film_w, film_m, film_v, small_w, small_m, small_v,
):
    n_dp, n_ch = lax.axis_size("dp"), lax.axis_size("chan")
    lens = lengths.reshape(1, -1)

    def taps_first(*arrays):
        return tuple(jnp.transpose(a, (1, 0, 2)) for a in arrays)

    one, two, down = (
        taps_first(*state) for state in ((conv1_w, conv1_m, conv1_v), (conv2_w, conv2_m, conv2_v), (down_w, down_m, down_v))
    )
    cond, film_rows = condition, film_w
    frows = film_w.shape[0]
    if frows % 16:
        short = -frows % 16
        film_rows = jnp.pad(film_w, ((0, short), (0, 0), (0, 0)))
        cond = jnp.pad(condition.reshape(-1, n_dp, frows), ((0, 0), (0, 0), (0, short))).reshape(condition.shape[0], -1)
    output, input_grad, gw, gf, gs = block_step(
        n_dp, n_ch, inputs, cotangent, cond, lens, one[0], two[0], res_w, down[0], film_rows, small_w
    )
    output, input_grad, *state = update(
        output, input_grad, gw, gf, gs, *one, *two, res_w, res_m, res_v, *down, film_w, film_m, film_v, small_w, small_m, small_v
    )
    state = (*taps_first(*state[:6]), *state[6:9], *taps_first(*state[9:12]), *state[12:])
    return (output, input_grad, *state)


def solution(mesh):
    in_specs = (
        P("dp", "chan"),
        P("dp", None),
        P("dp"),
        P("dp", "chan"),
        P("dp", None, "chan"),
        P("dp", None, "chan"),
        P("dp", None, "chan"),
        P("dp", None, "chan"),
        P("dp", None, "chan"),
        P("dp", None, "chan"),
        P("dp", "chan"),
        P("dp", "chan"),
        P("dp", "chan"),
        P("dp", None, "chan"),
        P("dp", None, "chan"),
        P("dp", None, "chan"),
        P("dp", None, "chan"),
        P("dp", None, "chan"),
        P("dp", None, "chan"),
        P(None, "chan"),
        P(None, "chan"),
        P(None, "chan"),
    )
    out_specs = (
        P("dp", "chan"),
        P("dp", "chan"),
        P("dp", None, "chan"),
        P("dp", None, "chan"),
        P("dp", None, "chan"),
        P("dp", None, "chan"),
        P("dp", None, "chan"),
        P("dp", None, "chan"),
        P("dp", "chan"),
        P("dp", "chan"),
        P("dp", "chan"),
        P("dp", None, "chan"),
        P("dp", None, "chan"),
        P("dp", None, "chan"),
        P("dp", None, "chan"),
        P("dp", None, "chan"),
        P("dp", None, "chan"),
        P(None, "chan"),
        P(None, "chan"),
        P(None, "chan"),
    )
    return jax.shard_map(body, mesh=mesh, in_specs=in_specs, out_specs=out_specs, check_vma=False)
```

time: 203 us -> 124 us (0.61)
  Pallas kernels: 169 us -> 123 us
  local copies, waits for them, and re-layouts: 32.3 us -> 0 us
    pallas_call x1, Pallas kernels: 165 us -> 119 us  [block_step(): pl.pallas_call(partial(step_kernel, n_dp, n_ch), out_shape=out, in_specs=...]
    unnamed x74 -> x0, local copies, waits for them, and re-layouts: 30.8 us -> none
where the time goes in v2:
time: 124 us
  Pallas kernels  123 us (99%)
    pallas_call x1, Pallas kernels, block_step(): pl.pallas_call(partial(step_kernel, n_dp, n_ch), out_shape=out, in_specs=...  119 us
    pallas_call x1, Pallas kernels, update(): pl.pallas_call(partial(update_kernel, n), out_shape=[jax.ShapeDtypeStruct...  4.25 us

profile of v2, /device:TPU:0, one launch (start us, length us, event | category | flops | bytes accessed | tf_op | source)
XLA Modules:
  0.0 124.0 jit_solution(7449097148679580465)
XLA Ops:
  0.7 118.9 %block_step.1 = (bf16[2048,128]{1,0:T(8,128)(2,1)}, bf16[4096,128]{1,0:T(8,128)(2,1)}, f32[14,64,128]{2,1,0:T(8,128)}, f32[2,144,128]{2,1,0:T(8,128)}, f32[16,128]{1,0:T(8,128)}) custom-call(bf16[4096,128]{1,0:T(8,128)(2,1)} %inputs.1, bf16[2048,128]{1,0:T(8,128)(2,1)} %cot.1, f32[256,1152]{1,0:T(8,128)} %cond_h.1, s32[1,256]{1,0:T(1,128)} %bitcast.31, ...), custom_call_target="tpu_custom_call" | custom-call | tf_op jit(solution)/shard_map/block_step/pallas_call | solution.py:881
  119.6 4.3 %update.1 = (bf16[2048,128]{1,0:T(8,128)(2,1)}, bf16[4096,128]{1,0:T(8,128)(2,1)}, f32[5,64,128]{2,1,0:T(8,128)}, f32[5,64,128]{2,1,0:T(8,128)}, f32[5,64,128]{2...) custom-call(bf16[2048,128]{1,0:T(8,128)(2,1)} %get-tuple-element.45., ...), custom_call_target="tpu_custom_call" | custom-call | tf_op jit(solution)/shard_map/update/pallas_call | solution.py:968

commit v3 on v2

--- a/solution.py
+++ b/solution.py
@@ -62,10 +62,23 @@
 W_ONE, W_RES, W_TWO, W_DOWN = 0, TAPS, TAPS + 1, 2 * TAPS + 1
 N_TAPS = W_DOWN + DOWN
 PARTS = ((W_ONE, TAPS + 1), (W_TWO, TAPS), (W_DOWN, DOWN))
-G_DOWN, G_RES, G_TWO_A, G_TWO_B, G_ONE_A, G_ONE_B, G_ONE_C = range(7)
+GROUPS = ("DOWN", "RES", "TWO_A", "TWO_B", "ONE_A", "ONE_B", "ONE_C")
 SUMS = (
-    (W_DOWN, DOWN, True), (W_RES, 1, False), (W_TWO, 3, False), (W_TWO + 3, 2, True),
-    (W_ONE, 2, False), (W_ONE + 2, 2, False), (W_ONE + 4, 1, False),
+    (W_DOWN, 3, True),
+    (W_RES, 1, False),
+    (W_TWO, 3, False),
+    (W_TWO + 3, 2, True),
+    (W_ONE, 2, False),
+    (W_ONE + 2, 2, False),
+    (W_ONE + 4, 1, False),
+)
+BACKWARD = (
+    "gW_DOWN", "s_DOWN", "C2", "gblock", "gres", "gW_RES", "c_DOWN", "s_RES", "nb2", "gW_TWO_A", "c_RES",
+    "s_TWO_A", "cb2", "filmg", "c_TWO_A", "nb1", "x_RES", "downf", "gW_ONE_A", "s_ONE_A", "y_RES", "gW_ONE_C",
+    "fdot", "gW_TWO_B", "c_ONE_A", "small", "gW_ONE_B", "smy", "x_TWO_A", "s_ONE_C", "s_TWO_B", "cb1",
+    "s_ONE_B", "c_ONE_C", "smx", "c_TWO_B", "c_ONE_B", "y_DOWN", "y_TWO_A", "x_ONE_A", "x_ONE_C", "y_ONE_A",
+    "x_ONE_B", "y_TWO_B", "y_ONE_C", "ig", "x_DOWN", "z_ONE_C", "x_TWO_B", "z_DOWN", "y_ONE_B", "z_TWO_A",
+    "fz", "smz", "z_ONE_A", "z_ONE_B", "z_RES", "fe", "z_TWO_B", "sme",
 )
 SMALL = 16
 
@@ -78,7 +91,7 @@
     gfin, gffin, gsfin, rcb, rxb, ryb, sidebuf, rzb, rfx, rfz, rfs, gsm, gsr, cond, lens_row, lens_all, wraw, film_w, small_w,
     xpad, hpad, be, bo, cbuf, res, xh1, m1, dm1, xh2, dm2, gdn, gc2, gc1, gres,
     ag_send, ag_recv, st_send, st_recv, in_send, in_recv, fw_send, fw_recv, fo_send, fo_recv,
-    rs_send, rs_recv, rz_send, rz_recv, out_send, out_recv, gf_send, gf_recv, rf_send, rf_recv, gs_send, gs_recv, loc,
+    rs_send, rs_recv, out_send, out_recv, gf_send, gf_recv, rf_send, rf_recv, gs_send, gs_recv, loc,
 ):
     dp, ch = lax.axis_index("dp"), lax.axis_index("chan")
     hi, lo, yy, co = dp // 2, dp % 2, ch // 2, ch % 2
@@ -157,6 +170,14 @@
         stats[0, pl.ds(2 * feats, stats.shape[1] - 2 * feats), :] = jnp.zeros((stats.shape[1] - 2 * feats, 128), f32)
     pl.semaphore_wait(barrier, n_dp - 1 + n_ch - 1)
 
+    def arrived(ref, sem):
+        remote(ref, ref, sem, sem, (dp, ch)).wait_recv()
+
+    def gone(ref, sem):
+        remote(ref, ref, sem, sem, (dp, ch)).wait_send()
+
+    others = (n_ch - 1) * width
+
     far, near = hi // 2, hi % 2
     if n_hi == 4:
         line = (far * 2 + 1 - near, (1 - far) * 2 + far, (1 - far) * 3)
@@ -182,23 +203,24 @@
         t0, nt = PARTS[p]
         return w_all.at[pl.ds(t0, nt), at(d, rows), at(q, width)]
 
-    def pass_on(p, d, q, slot, device):
-        return remote(block(p, d, q), block(p, d, q), ag_send.at[p, slot], ag_recv.at[p, d, q], device)
+    def pass_on(p, d, q, s_at, r_at, device):
+        return remote(block(p, d, q), block(p, d, q), ag_send.at[p, s_at], ag_recv.at[p, r_at], device)
+
+    def to_z(p, h):
+        return pass_on(p, dp, ch, 0, hi, (h * 2 + lo, ch))
 
     def to_y(p, h):
-        return pass_on(p, h * 2 + lo, ch, n_hi + h, (dp, ch_y))
+        return pass_on(p, h * 2 + lo, ch, 1, n_hi + h, (dp, ch_y))
 
     def to_x(p, h, v):
-        return pass_on(p, h * 2 + lo, v * 2 + co, 2 * n_hi + 2 * h + v, (dp_x, ch))
+        return pass_on(p, h * 2 + lo, v * 2 + co, 2, 2 * n_hi + v, (dp_x, ch))
 
     def to_c(p, h, l, v):
-        return pass_on(p, h * 2 + l, v * 2 + co, 4 * n_hi + 4 * h + 2 * l + v, (dp, ch_c))
-
-    def to_z(p, h):
-        return pass_on(p, dp, ch, h, (h * 2 + lo, ch))
-
-    def landed(p, d, q):
-        pass_on(p, d, q, 0, (dp, ch)).wait_recv()
+        return pass_on(p, h * 2 + l, v * 2 + co, 3, 2 * n_hi + 2, (dp, ch_c))
+
+    def landed(p, n_rows, n_cols, at_sem):
+        t0, nt = PARTS[p]
+        arrived(w_all.at[pl.ds(t0, nt), pl.ds(0, n_rows), pl.ds(0, n_cols)], ag_recv.at[p, at_sem])
 
     def ag_far(p):
         along(lambda h: to_z(p, h).start())
@@ -209,20 +231,16 @@
         to_c(p, hi, lo, yy).start()
 
     def from_z(p, h):
-        landed(p, h * 2 + lo, ch)
+        landed(p, rows, width, h)
         to_y(p, h).start()
         to_x(p, h, yy).start()
         to_c(p, h, lo, yy).start()
 
     def from_y(p, h):
-        landed(p, h * 2 + lo, ch_y)
+        landed(p, rows, width, n_hi + h)
         to_x(p, h, 1 - yy).start()
         to_c(p, h, lo, 1 - yy).start()
 
-    def from_x(p, h, v):
-        landed(p, h * 2 + 1 - lo, v * 2 + co)
-        to_c(p, h, 1 - lo, v).start()
-
     def ag_z(p, middle=None):
         along(lambda h: from_z(p, h), middle)
 
@@ -231,75 +249,60 @@
 
     def ag_x(p):
         for v in (yy, 1 - yy):
-            from_x(p, hi, v)
-            along(lambda h: from_x(p, h, v))
+            landed(p, n_hi * rows, width, 2 * n_hi + v)
+
+            @pl.loop(0, n_hi)
+            def _(h):
+                to_c(p, h, 1 - lo, v).start()
 
     def ag_core(p):
-        @pl.loop(0, n_dp)
-        def _(d):
-            for v in range(n_ch // 2):
-                landed(p, d, v * 2 + 1 - co)
+        landed(p, c, 2 * width, 2 * n_hi + 2)
 
     def ag_done(p):
-        along(lambda h: to_z(p, h).wait_send())
-
-        @pl.loop(0, n_hi)
-        def _(h):
-            to_y(p, h).wait_send()
-            for v in range(2):
-                to_x(p, h, v).wait_send()
-                for l in range(2):
-                    to_c(p, h, l, v).wait_send()
+        t0, nt = PARTS[p]
+        for i, (n_rows, n_cols) in enumerate((((n_hi - 1) * rows, width), (n_hi * rows, width), (c, width), (c, 2 * width))):
+            gone(w_all.at[pl.ds(t0, nt), pl.ds(0, n_rows), pl.ds(0, n_cols)], ag_send.at[p, i])
 
     def swap_in(src, dst, n, k, i):
         q = (ch + i) % n_ch
-        return remote(src.at[at(q, n)], dst.at[:, my_cols], in_send.at[k, i], in_recv.at[k, i], (dp, q))
-
-    def swap_in_wait(src, dst, n, k):
-        for i in range(1, n_ch):
-            q = (ch + n_ch - i) % n_ch
-            remote(src.at[at(q, n)], dst.at[:, at(q, width)], in_send.at[k, i], in_recv.at[k, i], (dp, q)).wait_recv()
-        for i in range(1, n_ch):
-            swap_in(src, dst, n, k, i).wait_send()
+        return remote(src.at[at(q, n)], dst.at[:, my_cols], in_send.at[k], in_recv.at[k], (dp, q))
+
+    def swap_in_wait(dst, k):
+        arrived(dst.at[:, pl.ds(0, others)], in_recv.at[k])
+        gone(dst.at[:, pl.ds(0, others)], in_send.at[k])
 
     def swap_out(src, dst, n, k, i):
         q = (ch + i) % n_ch
-        return remote(src.at[:, at(q, width)], dst.at[at(ch, n)], out_send.at[k, i], out_recv.at[k, i], (dp, q))
+        return remote(src.at[:, at(q, width)], dst.at[at(ch, n)], out_send.at[k], out_recv.at[k], (dp, q))
 
     def swap_out_wait(src, dst, n, k):
-        for i in range(1, n_ch):
-            q = (ch + n_ch - i) % n_ch
-            remote(src.at[:, at(q, width)], dst.at[at(q, n)], out_send.at[k, i], out_recv.at[k, i], (dp, q)).wait_recv()
-        for i in range(1, n_ch):
-            swap_out(src, dst, n, k, i).wait_send()
-
-    def small_swap(i, q):
-        return remote(small.at[:, at(q, width)], small.at[:, at(q, width)], in_send.at[2, i], in_recv.at[2, i], (dp, (ch + i) % n_ch))
+        arrived(dst.at[pl.ds(0, (n_ch - 1) * n)], out_recv.at[k])
+        gone(src.at[:, pl.ds(0, others)], out_send.at[k])
+
+    def small_swap(i):
+        return remote(small.at[:, my_cols], small.at[:, my_cols], in_send.at[2], in_recv.at[2], (dp, (ch + i) % n_ch))
 
     def bounds_x():
-        return remote(stats.at[0], stats.at[1], st_send.at[n_hi], st_recv.at[n_hi], (dp_x, ch))
+        return remote(stats.at[0], stats.at[1], st_send.at[0], st_recv.at[0], (dp_x, ch))
 
     def bounds_z(h):
-        return remote(stats.at[2], stats.at[3 + hi], st_send.at[h], st_recv.at[hi], (h * 2 + lo, ch))
-
-    def bounds_in(h):
-        return remote(stats.at[2], stats.at[3 + h], st_send.at[h], st_recv.at[h], (h * 2 + lo, ch))
+        return remote(stats.at[2], stats.at[3 + hi], st_send.at[1], st_recv.at[1], (h * 2 + lo, ch))
 
     def film_block(d):
         return wf_all.at[:, at(d, frp), :]
 
-    def film_pass(d, slot, device):
-        return remote(film_block(d), film_block(d), fw_send.at[slot], fw_recv.at[d], device)
+    def film_pass(d, at_sem, device):
+        return remote(film_block(d), film_block(d), fw_send.at[at_sem], fw_recv.at[at_sem], device)
 
     def film_x():
         return film_pass(dp, 0, (dp_x, ch))
 
     def film_z(i, l):
-        return film_pass(hi * 2 + l, 2 * i + l, ((hi + i) % n_hi * 2 + lo, ch))
+        return film_pass(hi * 2 + l, 1, ((hi + i) % n_hi * 2 + lo, ch))
 
     def film_swap(i, q):
         return remote(
-            film_out.at[:, at(q, s), :], film.at[:, :, my_cols], fo_send.at[i], fo_recv.at[i], (dp, q)
+            film_out.at[:, at(q, s), :], film.at[:, :, my_cols], fo_send.at[0], fo_recv.at[0], (dp, q)
         )
 
     bounds_x().start()
@@ -308,7 +311,7 @@
     ag_own(0)
     ag_own(1)
     for i in range(1, n_ch):
-        small_swap(i, ch).start()
+        small_swap(i).start()
     bounds_x().wait_recv()
     stats[2] = jnp.maximum(stats[0], stats[1])
     stats[3 + hi] = stats[2]
@@ -319,7 +322,7 @@
         swap_in(inputs, x_raw, m, 0, i).start()
     from_y(1, hi)
     ag_y(0)
-    along(lambda h: bounds_in(h).wait_recv())
+    arrived(stats.at[pl.ds(3, n_hi - 1)], st_recv.at[1])
     best = stats[3]
     for h in range(1, n_hi):
         best = jnp.maximum(best, stats[3 + h])
@@ -352,7 +355,7 @@
 
     count = wide(lens_ref[...].astype(f32), c) * GROUP
     own_x.wait()
-    swap_in_wait(inputs, x_raw, m, 0)
+    swap_in_wait(x_raw, 0)
     sb = 256 // frames
     turn = grid_turn(sb, frames)
     for b in range(s // sb):
@@ -411,13 +414,9 @@
     ag_y(1)
     ag_own(2)
     conv_fwd(xpad, W_ONE, keep_c)
-    for i in range(1, n_ch):
-        small_swap(i, (ch + n_ch - i) % n_ch).wait_recv()
+    arrived(small.at[:, pl.ds(0, others)], in_recv.at[2])
     bias = row(0)
-    @pl.loop(1, n_hi)
-    def _(i):
-        for l in range(2):
-            film_pass((hi + i) % n_hi * 2 + l, 0, (dp, ch)).wait_recv()
+    arrived(wf_all.at[:, pl.ds(0, 2 * (n_hi - 1) * frp), :], fw_recv.at[1])
 
     for i in range(2):
         film_out[i] = dot_nn(act[...], wf_all[i]) + small[pl.ds(6 + i, 1), my_cols]
@@ -435,9 +434,7 @@
     ag_x(1)
     for i in range(1, n_ch):
         swap_in(cot, cot_raw, h2, 1, i).start()
-    for i in range(1, n_ch):
-        q = (ch + n_ch - i) % n_ch
-        remote(film_out.at[:, at(q, s), :], film.at[:, :, at(q, width)], fo_send.at[i], fo_recv.at[i], (dp, q)).wait_recv()
+    arrived(film.at[:, :, pl.ds(0, others)], fo_recv.at[0])
     for t in range(frames):
         part = pl.ds(t * s, s)
         xh = (cbuf[part, :] + bias - mean) * rstd1
@@ -473,7 +470,7 @@
     taps_at = (0, 0, s)
     ag_x(2)
     own_cot.wait()
-    swap_in_wait(cot, cot_raw, h2, 1)
+    swap_in_wait(cot_raw, 1)
     for b in range(s // sh):
         y = dot_nn(turn_h, cot_raw[pl.ds(b * 256, 256), :])
         lens_b = lens_ref[pl.ds(b * sh, sh), :]
@@ -491,7 +488,7 @@
         return remote(
             gw_all.at[pl.ds(t0, nt), :, at(v * 2 + 1 - co, width)],
             rcb.at[pl.ds(t0, nt), :, pl.ds(v * width, width)],
-            rs_send.at[p, v], rs_recv.at[p, v], (dp, ch_c),
+            rs_send.at[p, 0], rs_recv.at[p, 0], (dp, ch_c),
         )
 
     def rs_x(p, h):
@@ -502,7 +499,7 @@
         return remote(
             src.at[pl.ds(t1, nt), at(h * 2 + 1 - lo, rows), :],
             dst.at[pl.ds(t0, nt), at(h, rows), :],
-            rz_send.at[p, n_hi + h], rz_recv.at[p, n_hi + h], (dp_x, ch),
+            rs_send.at[p, 1], rs_recv.at[p, 1], (dp_x, ch),
         )
 
     def rs_y(p):
@@ -515,7 +512,7 @@
         t0, nt, y_first = SUMS[p]
         h = (hi + i) % n_hi
         return remote(
-            ryb.at[pl.ds(t0, nt), at(h, rows), :], rzb.at[i, pl.ds(t0, nt)], rz_send.at[p, i], rz_recv.at[p, i], (h * 2 + lo, ch)
+            ryb.at[pl.ds(t0, nt), at(h, rows), :], rzb.at[i, pl.ds(t0, nt)], rs_send.at[p, 3], rs_recv.at[p, 3], (h * 2 + lo, ch)
         )
 
     def rs_start(p):
@@ -536,8 +533,9 @@
             rs_z(p, i).start()
 
     def rs_after_core(p):
-        for v in range(2):
-            rs_core(p, v).wait()
+        both = rcb.at[pl.ds(SUMS[p][0], SUMS[p][1])]
+        arrived(both, rs_recv.at[p, 0])
+        gone(both, rs_send.at[p, 0])
 
         @pl.loop(SUMS[p][0], SUMS[p][0] + SUMS[p][1])
         def _(k):
@@ -553,9 +551,9 @@
     def rs_after_x(p):
         t0 = SUMS[p][0]
 
-        @pl.loop(0, n_hi)
-        def _(h):
-            rs_x(p, h).wait()
+        every = (ryb if SUMS[p][2] else rxb).at[pl.ds(t0, SUMS[p][1])]
+        arrived(every, rs_recv.at[p, 1])
+        gone(every, rs_send.at[p, 1])
 
         @pl.loop(SUMS[p][0], SUMS[p][0] + SUMS[p][1])
         def _(k):
@@ -591,9 +589,9 @@
     def rs_after_z(p):
         t0, nt, y_first = SUMS[p]
 
-        @pl.loop(1, n_hi)
-        def _(i):
-            rs_z(p, i).wait()
+        every = rzb.at[pl.ds(1, n_hi - 1), pl.ds(t0, nt)]
+        arrived(every, rs_recv.at[p, 3])
+        gone(every, rs_send.at[p, 3])
 
         @pl.loop(t0, t0 + nt)
         def _(k):
@@ -604,55 +602,7 @@
 
         results.append(local(12 + p, gfin.at[pl.ds(t0, nt)], gfin_h.at[pl.ds(t0, nt)]))
 
-    for k in range(DOWN):
-        for n in range(c // NB):
-            cols = pl.ds(n * NB, NB)
-            gw_all[dbase + k, :, cols] = dot_tn(taps_in[k][pl.ds(taps_at[k], hm), :], gdn[pl.ds(0, hm), cols]).astype(bf16)
-    rs_start(G_DOWN)
-    ag_core(2)
-    for n in range(c // NB):
-        cols = pl.ds(n * NB, NB)
-        acc = dot_nn(bo[pl.ds(0, hm), :], w_all[dbase, :, cols])
-        acc += dot_nn(be[...], w_all[dbase + 1, :, cols])
-        acc += dot_nn(bo[pl.ds(s, hm), :], w_all[dbase + 2, :, cols])
-        obuf[:, cols] = acc
-    for b in range(s // sh):
-        pieces = []
-        lens_b = lens_ref[pl.ds(b * sh, sh), :]
-        for j in range(half):
-            keep = wide((lens_b > 2 * j).astype(f32), c)
-            pieces.append(((obuf[pl.ds(j * s + b * sh, sh), :] + row(9)) * keep).astype(bf16))
-        out_raw[pl.ds(b * 256, 256), :] = dot_nn(back_h, jnp.concatenate(pieces, axis=0)).astype(bf16)
-    for i in range(1, n_ch):
-        swap_out(out_raw, output, h2, 0, i).start()
-    own_out = local(2, out_raw.at[:, my_cols], output.at[at(ch, h2)])
-
-    for n in range(c // NB):
-        cols = pl.ds(n * NB, NB)
-        ge = dot_nt(gdn[pl.ds(0, hm), :], w_all[dbase + 1, cols, :])
-        go = dot_nt(gdn[pl.ds(0, hm), :], w_all[dbase + 2, cols, :])
-        go += dot_nt(gdn[pl.ds(s, hm), :], w_all[dbase, cols, :])
-        for j in range(half):
-            cbuf[pl.ds(2 * j * s, s), cols] = ge[j * s : (j + 1) * s]
-            cbuf[pl.ds((2 * j + 1) * s, s), cols] = go[j * s : (j + 1) * s]
-
-    rs_after_core(G_DOWN)
-    tot = jnp.zeros((s, c), f32)
-    for j in range(half):
-        tot += gdn[pl.ds(j * s, s), :].astype(f32)
     gs = [None] * SMALL
-    gs[9] = jnp.sum(tot, axis=0, keepdims=True)
-    tot = jnp.zeros((s, c), f32)
-    for t in range(frames):
-        part = pl.ds(t * s, s)
-        g = cbuf[part, :] * mask(t)
-        tot += g
-        gres[part, :] = g.astype(bf16)
-    gs[8] = jnp.sum(tot, axis=0, keepdims=True)
-    for n in range(c // NB):
-        cols = pl.ds(n * NB, NB)
-        gw_all[W_RES, :, cols] = dot_tn(xpad[pl.ds(2 * s, m), :], gres[:, cols]).astype(bf16)
-    rs_start(G_RES)
 
     def norm_back(xh, dm, gain, rstd, dst, scale):
         a1 = jnp.zeros((s, c), f32)
@@ -675,165 +625,216 @@
             dst[pl.ds((t + 2) * s, s), :] = dp_t.astype(bf16)
         return [jnp.sum(v, axis=0, keepdims=True) for v in (tot, a2, a1)]
 
-    gs[3:6] = norm_back(xh2, dm2, row(4), rstd2, gc2, None)
-    rs_after_core(G_RES)
-    conv_bwd(gc2, W_TWO, keep_c)
-    tot1 = jnp.zeros((s, c), f32)
-    tot2 = jnp.zeros((s, c), f32)
-    for t in range(frames):
-        part = pl.ds(t * s, s)
-        g = cbuf[part, :] * mask(t)
-        tot1 += g * m1[part, :]
-        tot2 += g
-    gfilm[0] = tot1.astype(bf16)
-    gfilm[1] = tot2.astype(bf16)
-    gs[6] = jnp.sum(tot1, axis=0, keepdims=True)
-    gs[7] = jnp.sum(tot2, axis=0, keepdims=True)
-
     def film_back(i):
         q = (ch + i) % n_ch
-        return remote(gfilm.at[:, :, at(q, width)], gfa.at[:, at(ch, s), :], gf_send.at[i], gf_recv.at[i], (dp, q))
-
-    for i in range(1, n_ch):
-        film_back(i).start()
-    gfa[:, at(ch, s), :] = gfilm[:, :, my_cols]
-    conv_grad(hpad, gc2, W_TWO, 0, 3)
-    rs_start(G_TWO_A)
-    conv_grad(hpad, gc2, W_TWO, 3, TAPS)
-    rs_start(G_TWO_B)
-    rs_after_core(G_TWO_A)
-    gs[0:3] = norm_back(xh1, dm1, row(1), rstd1, gc1, film[0])
-    for i in range(1, n_ch):
-        q = (ch + n_ch - i) % n_ch
-        remote(gfilm.at[:, :, at(q, width)], gfa.at[:, at(q, s), :], gf_send.at[i], gf_recv.at[i], (dp, q)).wait_recv()
-    for i in range(2):
-        gwf[i] = dot_tn(act[...], gfa[i]).astype(bf16)
+        return remote(gfilm.at[:, :, at(q, width)], gfa.at[:, at(ch, s), :], gf_send.at[0], gf_recv.at[0], (dp, q))
+
+    def small_c():
+        return remote(gsm, gsr.at[0], gs_send.at[0], gs_recv.at[0], (dp, ch_c))
+
+    def small_y():
+        cols = at(ch_y, width)
+        return remote(gsm.at[:, cols], gsr.at[1, :, cols], gs_send.at[1], gs_recv.at[1], (dp, ch_y))
+
+    def small_x():
+        return remote(gsm.at[:, my_cols], gsr.at[2, :, my_cols], gs_send.at[2], gs_recv.at[2], (dp_x, ch))
+
+    def small_z(i):
+        device = ((hi + i) % n_hi * 2 + lo, ch)
+        return remote(gsm.at[:, my_cols], gsr.at[2 + i, :, my_cols], gs_send.at[3], gs_recv.at[3], device)
+
+    def keep_ig(part, cols, acc):
+        cbuf[part, cols] = acc + dot_nt(gres[part, :], w_all[W_RES, cols, :])
 
     def rf_z(i):
         h = (hi + i) % n_hi
-        return remote(gwf.at[:, at(h, 2 * frp), :], rfz.at[i], rf_send.at[i], rf_recv.at[i], (h * 2 + lo, ch))
+        return remote(gwf.at[:, at(h, 2 * frp), :], rfz.at[i], rf_send.at[0], rf_recv.at[0], (h * 2 + lo, ch))
 
     def rf_x():
-        return remote(rfs.at[:, at(1 - lo, frp), :], rfx, rf_send.at[0], rf_recv.at[0], (dp_x, ch))
-
-    @pl.loop(1, n_hi)
-    def _(i):
-        rf_z(i).start()
-
-    rs_after_core(G_TWO_B)
-    rs_after_y(G_DOWN)
-    rs_after_x(G_RES)
-    zero = jnp.zeros((1, c), f32)
-    for i in range(SMALL):
-        gsm[pl.ds(i, 1), :] = gs[i] if gs[i] is not None else zero
-
-    def small_pass(i, device):
-        return remote(gsm, gsr.at[i], gs_send.at[i], gs_recv.at[i], device)
-
-    small_pass(0, (dp, ch_c)).start()
-    def keep_ig(part, cols, acc):
-        cbuf[part, cols] = acc + dot_nt(gres[part, :], w_all[W_RES, cols, :])
-
-    conv_bwd(gc1, W_ONE, keep_ig)
-    back = grid_turn(frames, sb)
-    for b in range(s // sb):
-        lens_b = lens_ref[pl.ds(b * sb, sb), :]
-        pieces = [
-            (cbuf[pl.ds(t * s + b * sb, sb), :] * wide((lens_b > t).astype(f32), c)).astype(bf16) for t in range(frames)
-        ]
-        ig_raw[pl.ds(b * 256, 256), :] = dot_nn(back, jnp.concatenate(pieces, axis=0)).astype(bf16)
-    rs_after_x(G_TWO_A)
-    for i in range(1, n_ch):
-        swap_out(ig_raw, input_grad, m, 1, i).start()
-    own_ig = local(3, ig_raw.at[:, my_cols], input_grad.at[at(ch, m)])
-
-    small_pass(0, (dp, ch_c)).wait()
-    gsm[...] += gsr[0]
-    small_pass(1, (dp_x, ch)).start()
-    conv_grad(xpad, gc1, W_ONE, 0, 2)
-    rs_start(G_ONE_A)
-    rs_after_y(G_TWO_B)
-    conv_grad(xpad, gc1, W_ONE, 2, 4)
-    rs_start(G_ONE_B)
-    rs_after_core(G_ONE_A)
-    rs_after_x(G_DOWN)
-    conv_grad(xpad, gc1, W_ONE, 4, 5)
-    rs_start(G_ONE_C)
-    rs_after_core(G_ONE_B)
-    rs_after_y(G_RES)
-    rs_after_core(G_ONE_C)
-    small_pass(1, (dp_x, ch)).wait()
-    gsm[...] += gsr[1]
-    small_pass(2, (dp, ch_y)).start()
-    rs_after_y(G_TWO_A)
-    rs_after_x(G_TWO_B)
-    @pl.loop(1, n_hi)
-    def _(i):
-        rf_z(i).wait()
-
-    for v in range(2):
-        def more(i, tot):
-            return tot + rfz[i, v].astype(f32)
-
-        rfs[v] = lax.fori_loop(1, n_hi, more, gwf[v, at(hi, 2 * frp), :].astype(f32)).astype(bf16)
-    rf_x().start()
+        return remote(rfs.at[:, at(1 - lo, frp), :], rfx, rf_send.at[1], rf_recv.at[1], (dp_x, ch))
+
+    def gw_down():
+        for k in range(DOWN):
+            for n in range(c // NB):
+                cols = pl.ds(n * NB, NB)
+                gw_all[dbase + k, :, cols] = dot_tn(taps_in[k][pl.ds(taps_at[k], hm), :], gdn[pl.ds(0, hm), cols]).astype(bf16)
+
+    def gw_res():
+        for n in range(c // NB):
+            cols = pl.ds(n * NB, NB)
+            gw_all[W_RES, :, cols] = dot_tn(xpad[pl.ds(2 * s, m), :], gres[:, cols]).astype(bf16)
+
+    def result_rows():
+        for n in range(c // NB):
+            cols = pl.ds(n * NB, NB)
+            acc = dot_nn(bo[pl.ds(0, hm), :], w_all[dbase, :, cols])
+            acc += dot_nn(be[...], w_all[dbase + 1, :, cols])
+            acc += dot_nn(bo[pl.ds(s, hm), :], w_all[dbase + 2, :, cols])
+            obuf[:, cols] = acc
+        for b in range(s // sh):
+            pieces = []
+            lens_b = lens_ref[pl.ds(b * sh, sh), :]
+            for j in range(half):
+                keep = wide((lens_b > 2 * j).astype(f32), c)
+                pieces.append(((obuf[pl.ds(j * s + b * sh, sh), :] + row(9)) * keep).astype(bf16))
+            out_raw[pl.ds(b * 256, 256), :] = dot_nn(back_h, jnp.concatenate(pieces, axis=0)).astype(bf16)
+        for i in range(1, n_ch):
+            swap_out(out_raw, output, h2, 0, i).start()
+        results.append(local(2, out_raw.at[:, my_cols], output.at[at(ch, h2)]))
+
+    def into_block():
+        for n in range(c // NB):
+            cols = pl.ds(n * NB, NB)
+            ge = dot_nt(gdn[pl.ds(0, hm), :], w_all[dbase + 1, cols, :])
+            go = dot_nt(gdn[pl.ds(0, hm), :], w_all[dbase + 2, cols, :])
+            go += dot_nt(gdn[pl.ds(s, hm), :], w_all[dbase, cols, :])
+            for j in range(half):
+                cbuf[pl.ds(2 * j * s, s), cols] = ge[j * s : (j + 1) * s]
+                cbuf[pl.ds((2 * j + 1) * s, s), cols] = go[j * s : (j + 1) * s]
+
+    def into_res():
+        tot = jnp.zeros((s, c), f32)
+        for j in range(half):
+            tot += gdn[pl.ds(j * s, s), :].astype(f32)
+        gs[9] = jnp.sum(tot, axis=0, keepdims=True)
+        tot = jnp.zeros((s, c), f32)
+        for t in range(frames):
+            part = pl.ds(t * s, s)
+            g = cbuf[part, :] * mask(t)
+            tot += g
+            gres[part, :] = g.astype(bf16)
+        gs[8] = jnp.sum(tot, axis=0, keepdims=True)
+
+    def norm_back_two():
+        gs[3:6] = norm_back(xh2, dm2, row(4), rstd2, gc2, None)
+
+    def norm_back_one():
+        gs[0:3] = norm_back(xh1, dm1, row(1), rstd1, gc1, film[0])
+
+    def film_rows():
+        tot1 = jnp.zeros((s, c), f32)
+        tot2 = jnp.zeros((s, c), f32)
+        for t in range(frames):
+            part = pl.ds(t * s, s)
+            g = cbuf[part, :] * mask(t)
+            tot1 += g * m1[part, :]
+            tot2 += g
+        gfilm[0] = tot1.astype(bf16)
+        gfilm[1] = tot2.astype(bf16)
+        gs[6] = jnp.sum(tot1, axis=0, keepdims=True)
+        gs[7] = jnp.sum(tot2, axis=0, keepdims=True)
+
+        for i in range(1, n_ch):
+            film_back(i).start()
+        gfa[:, at(ch, s), :] = gfilm[:, :, my_cols]
+
+    def film_start():
+        arrived(gfa.at[:, pl.ds(0, (n_ch - 1) * s), :], gf_recv.at[0])
+        for i in range(2):
+            gwf[i] = dot_tn(act[...], gfa[i]).astype(bf16)
+
+        @pl.loop(1, n_hi)
+        def _(i):
+            rf_z(i).start()
+
+    def film_hi():
+        arrived(rfz.at[pl.ds(1, n_hi - 1)], rf_recv.at[0])
+        gone(rfz.at[pl.ds(1, n_hi - 1)], rf_send.at[0])
+
+        for v in range(2):
+            def more(i, tot):
+                return tot + rfz[i, v].astype(f32)
+
+            rfs[v] = lax.fori_loop(1, n_hi, more, gwf[v, at(hi, 2 * frp), :].astype(f32)).astype(bf16)
+        rf_x().start()
+
+    def film_end():
+        rf_x().wait()
+        for v in range(2):
+            gffin[v] = rfs[v, at(lo, frp), :].astype(f32) + rfx[v].astype(f32)
+        results.append(local(12 + len(SUMS), gffin, gffin_h))
+
+    def small_start():
+        zero = jnp.zeros((1, c), f32)
+        for i in range(SMALL):
+            gsm[pl.ds(i, 1), :] = gs[i] if gs[i] is not None else zero
+
+        small_c().start()
+
+    def small_to_y():
+        small_c().wait()
+        gsm[...] += gsr[0]
+        small_y().start()
+
+    def small_to_x():
+        small_y().wait()
+        gsm[:, my_cols] += gsr[1, :, my_cols]
+        small_x().start()
+
+    def small_to_z():
+        small_x().wait()
+        gsm[:, my_cols] += gsr[2, :, my_cols]
+
+        @pl.loop(1, n_hi)
+        def _(i):
+            small_z(i).start()
+
+    def small_end():
+        arrived(gsr.at[pl.ds(3, n_hi - 1), :, my_cols], gs_recv.at[3])
+        gone(gsr.at[pl.ds(3, n_hi - 1), :, my_cols], gs_send.at[3])
+
+        def more_small(i, tot):
+            return tot + gsr[2 + i, :, my_cols]
+
+        gsfin[...] = lax.fori_loop(1, n_hi, more_small, gsm[:, my_cols])
+        results.append(local(13 + len(SUMS), gsfin, gsfin_h))
+
+    def input_rows():
+        back = grid_turn(frames, sb)
+        for b in range(s // sb):
+            lens_b = lens_ref[pl.ds(b * sb, sb), :]
+            pieces = [
+                (cbuf[pl.ds(t * s + b * sb, sb), :] * wide((lens_b > t).astype(f32), c)).astype(bf16) for t in range(frames)
+            ]
+            ig_raw[pl.ds(b * 256, 256), :] = dot_nn(back, jnp.concatenate(pieces, axis=0)).astype(bf16)
+        for i in range(1, n_ch):
+            swap_out(ig_raw, input_grad, m, 1, i).start()
+        results.append(local(3, ig_raw.at[:, my_cols], input_grad.at[at(ch, m)]))
+
+    def weight_grad(name):
+        t0, nt, _ = SUMS[GROUPS.index(name)]
+        src, g, first = (hpad, gc2, W_TWO) if name.startswith("TWO") else (xpad, gc1, W_ONE)
+        conv_grad(src, g, first, t0 - first, t0 - first + nt)
+
+    steps = dict(
+        C2=lambda: ag_core(2), downf=result_rows, gW_DOWN=gw_down, gW_RES=gw_res, gblock=into_block, gres=into_res,
+        nb2=norm_back_two, nb1=norm_back_one, filmg=film_rows, fdot=film_start, fz=film_hi, fe=film_end,
+        small=small_start, smy=small_to_y, smx=small_to_x, smz=small_to_z, sme=small_end,
+        cb2=lambda: conv_bwd(gc2, W_TWO, keep_c), cb1=lambda: conv_bwd(gc1, W_ONE, keep_ig), ig=input_rows,
+    )
+    sums = dict(s=rs_start, c=rs_after_core, x=rs_after_x, y=rs_after_y, z=rs_after_z)
+    for name in BACKWARD:
+        kind, _, group = name.partition("_")
+        if name in steps:
+            steps[name]()
+        elif kind == "gW":
+            weight_grad(group)
+        else:
+            sums[kind](GROUPS.index(group))
     for p in range(3):
         ag_done(p)
     bounds_x().wait_send()
-    along(lambda h: bounds_z(h).wait_send())
-
-    @pl.loop(1, n_hi)
-    def _(i):
-        for l in range(2):
-            film_z(i, l).wait_send()
+    gone(stats.at[pl.ds(3, n_hi - 1)], st_send.at[1])
+
+    gone(wf_all.at[:, pl.ds(0, 2 * (n_hi - 1) * frp), :], fw_send.at[1])
 
     film_x().wait_send()
-    for i in range(1, n_ch):
-        small_swap(i, ch).wait_send()
-        film_swap(i, (ch + i) % n_ch).wait_send()
-        film_back(i).wait_send()
-    rs_after_z(G_RES)
-    rs_after_z(G_DOWN)
-    rs_after_x(G_ONE_A)
-    rs_after_z(G_TWO_B)
-    rs_after_x(G_ONE_B)
-    small_pass(2, (dp, ch_y)).wait()
-    gsm[...] += gsr[2]
-
-    def small_z(i):
-        return small_pass(2 + i, ((hi + i) % n_hi * 2 + lo, ch))
-
-    @pl.loop(1, n_hi)
-    def _(i):
-        small_z(i).start()
-
-    rs_after_y(G_ONE_A)
-    rs_after_x(G_ONE_C)
-    rs_after_z(G_TWO_A)
-    rf_x().wait()
-    for v in range(2):
-        gffin[v] = rfs[v, at(lo, frp), :].astype(f32) + rfx[v].astype(f32)
-    results.append(local(12 + len(SUMS), gffin, gffin_h))
-
-    rs_after_y(G_ONE_B)
-    rs_after_y(G_ONE_C)
-    rs_after_z(G_ONE_A)
-    @pl.loop(1, n_hi)
-    def _(i):
-        small_z(i).wait()
-
-    def more_small(i, tot):
-        return tot + gsr[2 + i, :, my_cols]
-
-    gsfin[...] = lax.fori_loop(1, n_hi, more_small, gsm[:, my_cols])
-    results.append(local(13 + len(SUMS), gsfin, gsfin_h))
-    rs_after_z(G_ONE_B)
-    rs_after_z(G_ONE_C)
+    gone(small.at[:, pl.ds(0, others)], in_send.at[2])
+    gone(film.at[:, :, pl.ds(0, others)], fo_send.at[0])
+    gone(gfa.at[:, pl.ds(0, (n_ch - 1) * s), :], gf_send.at[0])
 
     for copy in results:
         copy.wait()
-    own_out.wait()
-    own_ig.wait()
     swap_out_wait(out_raw, output, h2, 0)
     swap_out_wait(ig_raw, input_grad, m, 1)
 
@@ -873,10 +874,9 @@
         pad, pad, V((h, c), bf16), V((h + s, c), bf16),
         full, full, full, full, full, full, full,
         V((h + s, c), bf16), pad, pad, V((m, c), bf16),
-        D((3, 8 * n_hi)), D((3, n_dp, n_ch)), D((n_hi + 1,)), D((n_hi + 1,)), D((3, n_ch)), D((3, n_ch)),
-        D((2 * n_hi,)), D((n_dp,)), D((n_ch,)), D((n_ch,)),
-        D((len(SUMS), 3)), D((len(SUMS), 3)), D((len(SUMS), 2 * n_hi)), D((len(SUMS), 2 * n_hi)), D((2, n_ch)), D((2, n_ch)), D((n_ch,)), D((n_ch,)),
-        D((n_hi,)), D((n_hi,)), D((2 + n_hi,)), D((2 + n_hi,)), D((14 + len(SUMS),)),
+        D((3, 4)), D((3, 2 * n_hi + 3)), D((2,)), D((2,)), D((3,)), D((3,)), D((2,)), D((2,)), D((1,)), D((1,)),
+        D((len(SUMS), 4)), D((len(SUMS), 4)), D((2,)), D((2,)), D((1,)), D((1,)), D((2,)), D((2,)), D((4,)), D((4,)),
+        D((14 + len(SUMS),)),
     ]
     return pl.pallas_call(
         partial(step_kernel, n_dp, n_ch),

time: 124 us -> 117 us (0.944)
  Pallas kernels: 123 us -> 116 us
    pallas_call x1, Pallas kernels: 119 us -> 112 us  [block_step(): pl.pallas_call(partial(step_kernel, n_dp, n_ch), out_shape=out, in_specs=...]
where the time goes in v3:
time: 117 us
  Pallas kernels  116 us (99%)
    pallas_call x1, Pallas kernels, block_step(): pl.pallas_call(partial(step_kernel, n_dp, n_ch), out_shape=out, in_specs=...  112 us
    pallas_call x1, Pallas kernels, update(): pl.pallas_call(partial(update_kernel, n), out_shape=[jax.ShapeDtypeStruct...  4.25 us

profile of v3, /device:TPU:0, one launch (start us, length us, event | category | flops | bytes accessed | tf_op | source)
XLA Modules:
  0.0 117.3 jit_solution(1669462796949268238)
XLA Ops:
  0.7 112.2 %block_step.1 = (bf16[2048,128]{1,0:T(8,128)(2,1)}, bf16[4096,128]{1,0:T(8,128)(2,1)}, f32[14,64,128]{2,1,0:T(8,128)}, f32[2,144,128]{2,1,0:T(8,128)}, f32[16,128]{1,0:T(8,128)}) custom-call(bf16[4096,128]{1,0:T(8,128)(2,1)} %inputs.1, bf16[2048,128]{1,0:T(8,128)(2,1)} %cot.1, f32[256,1152]{1,0:T(8,128)} %cond_h.1, s32[1,256]{1,0:T(1,128)} %bitcast.31, ...), custom_call_target="tpu_custom_call" | custom-call | tf_op jit(solution)/shard_map/block_step/pallas_call | solution.py:881
  112.9 4.3 %update.1 = (bf16[2048,128]{1,0:T(8,128)(2,1)}, bf16[4096,128]{1,0:T(8,128)(2,1)}, f32[5,64,128]{2,1,0:T(8,128)}, f32[5,64,128]{2,1,0:T(8,128)}, f32[5,64,128]{2...) custom-call(bf16[2048,128]{1,0:T(8,128)(2,1)} %get-tuple-element.45., ...), custom_call_target="tpu_custom_call" | custom-call | tf_op jit(solution)/shard_map/update/pallas_call | solution.py:968

commit v4 on v3

--- a/solution.py
+++ b/solution.py
@@ -59,26 +59,32 @@
 
 
 MESH = pl.DeviceIdType.MESH
-W_ONE, W_RES, W_TWO, W_DOWN = 0, TAPS, TAPS + 1, 2 * TAPS + 1
+W_ONE, W_TWO, W_RES, W_DOWN = 0, TAPS, 2 * TAPS, 2 * TAPS + 1
 N_TAPS = W_DOWN + DOWN
-PARTS = ((W_ONE, TAPS + 1), (W_TWO, TAPS), (W_DOWN, DOWN))
-GROUPS = ("DOWN", "RES", "TWO_A", "TWO_B", "ONE_A", "ONE_B", "ONE_C")
+PARTS = ((W_ONE, TAPS), (W_TWO, TAPS + 1), (W_DOWN, DOWN))
+GROUPS = ("DOWN", "RES", "TWO_A", "TWO_B", "TWO_C", "ONE_A", "ONE_B", "ONE_C")
 SUMS = (
-    (W_DOWN, 3, True),
-    (W_RES, 1, False),
-    (W_TWO, 3, False),
-    (W_TWO + 3, 2, True),
-    (W_ONE, 2, False),
-    (W_ONE + 2, 2, False),
-    (W_ONE + 4, 1, False),
+    (W_DOWN, 3, False),
+    (W_RES, 1, True),
+    (W_TWO, 1, True),
+    (W_TWO + 1, 2, False),
+    (W_TWO + 3, 2, False),
+    (W_ONE, 1, True),
+    (W_ONE + 1, 2, True),
+    (W_ONE + 3, 2, False),
 )
-BACKWARD = (
-    "gW_DOWN", "s_DOWN", "C2", "gblock", "gres", "gW_RES", "c_DOWN", "s_RES", "nb2", "gW_TWO_A", "c_RES",
-    "s_TWO_A", "cb2", "filmg", "c_TWO_A", "nb1", "x_RES", "downf", "gW_ONE_A", "s_ONE_A", "y_RES", "gW_ONE_C",
-    "fdot", "gW_TWO_B", "c_ONE_A", "small", "gW_ONE_B", "smy", "x_TWO_A", "s_ONE_C", "s_TWO_B", "cb1",
-    "s_ONE_B", "c_ONE_C", "smx", "c_TWO_B", "c_ONE_B", "y_DOWN", "y_TWO_A", "x_ONE_A", "x_ONE_C", "y_ONE_A",
-    "x_ONE_B", "y_TWO_B", "y_ONE_C", "ig", "x_DOWN", "z_ONE_C", "x_TWO_B", "z_DOWN", "y_ONE_B", "z_TWO_A",
-    "fz", "smz", "z_ONE_A", "z_ONE_B", "z_RES", "fe", "z_TWO_B", "sme",
+ORDER = (
+    "far0", "own0", "own1", "far1", "fx0", "own2", "fz0_1", "bx", "fy1_0", "fz0_2", "bz", "fz0_3", "fy0_2",
+    "inp", "fz1_2", "fy0_0", "filmon", "fy0_1", "far2", "fz1_3", "fz1_1", "fy0_3", "perm", "fy1_2", "fy1_3",
+    "xa0", "xb0", "cond", "core0", "smallin", "fy1_1", "fy2_0", "xa1", "fdotf", "conv1", "fz2_2", "st1",
+    "fz2_1", "fz2_3", "cot", "xb1", "app1", "core1", "fy2_2", "resd", "conv2", "fy2_1", "xa2", "st2", "fy2_3",
+    "app2", "xb2", "gdnp", "gW_DOWN", "s_DOWN", "C2", "gblock", "downf", "c_DOWN", "gres", "nb2", "gW_RES",
+    "s_RES", "gW_TWO_C", "s_TWO_C", "c_RES", "cb2", "filmg", "c_TWO_C", "nb1", "x_DOWN", "gW_ONE_A", "fdot",
+    "s_ONE_A", "y_RES", "small", "gW_ONE_C", "s_ONE_C", "smy", "c_ONE_A", "gW_TWO_B", "x_TWO_C", "c_ONE_C",
+    "gW_TWO_A", "s_TWO_A", "y_ONE_A", "s_TWO_B", "c_TWO_A", "gW_ONE_B", "s_ONE_B", "c_ONE_B", "y_TWO_C",
+    "c_TWO_B", "cb1", "fz", "x_ONE_C", "y_TWO_A", "y_DOWN", "x_TWO_B", "x_RES", "x_ONE_A", "x_TWO_A", "smx",
+    "y_ONE_C", "ig", "smz", "y_TWO_B", "y_ONE_B", "x_ONE_B", "z_TWO_C", "z_ONE_A", "z_ONE_C", "z_DOWN",
+    "z_TWO_A", "z_TWO_B", "fe", "sme", "z_RES", "z_ONE_B",
 )
 SMALL = 16
 
@@ -184,20 +190,15 @@
     else:
         line = None
 
-    def along(step, middle=None):
+    def along(step):
         if line is not None:
-            for j, h in enumerate(line):
+            for h in line:
                 step(h)
-                if j == 1 and middle is not None:
-                    middle()
         else:
 
             @pl.loop(1, n_hi)
             def _(i):
                 step((hi + i) % n_hi)
-
-            if middle is not None:
-                middle()
 
     def block(p, d, q):
         t0, nt = PARTS[p]
@@ -241,19 +242,21 @@
         to_x(p, h, 1 - yy).start()
         to_c(p, h, lo, 1 - yy).start()
 
-    def ag_z(p, middle=None):
-        along(lambda h: from_z(p, h), middle)
-
-    def ag_y(p):
-        along(lambda h: from_y(p, h))
-
-    def ag_x(p):
-        for v in (yy, 1 - yy):
-            landed(p, n_hi * rows, width, 2 * n_hi + v)
-
-            @pl.loop(0, n_hi)
-            def _(h):
-                to_c(p, h, 1 - lo, v).start()
+    passed = set()
+
+    def from_one(step, kind, p, j):
+        if line is not None:
+            step(p, line[j - 1])
+        elif (kind, p) not in passed:
+            passed.add((kind, p))
+            along(lambda h: step(p, h))
+
+    def from_x(p, v):
+        landed(p, n_hi * rows, width, 2 * n_hi + v)
+
+        @pl.loop(0, n_hi)
+        def _(h):
+            to_c(p, h, 1 - lo, v).start()
 
     def ag_core(p):
         landed(p, c, 2 * width, 2 * n_hi + 2)
@@ -305,66 +308,22 @@
             film_out.at[:, at(q, s), :], film.at[:, :, my_cols], fo_send.at[0], fo_recv.at[0], (dp, q)
         )
 
-    bounds_x().start()
-    film_x().start()
-    ag_far(0)
-    ag_own(0)
-    ag_own(1)
-    for i in range(1, n_ch):
-        small_swap(i).start()
-    bounds_x().wait_recv()
-    stats[2] = jnp.maximum(stats[0], stats[1])
-    stats[3 + hi] = stats[2]
-    along(lambda h: bounds_z(h).start())
-    from_y(0, hi)
-    ag_z(0, lambda: ag_far(1))
-    for i in range(1, n_ch):
-        swap_in(inputs, x_raw, m, 0, i).start()
-    from_y(1, hi)
-    ag_y(0)
-    arrived(stats.at[pl.ds(3, n_hi - 1)], st_recv.at[1])
-    best = stats[3]
-    for h in range(1, n_hi):
-        best = jnp.maximum(best, stats[3 + h])
-    low = -jnp.concatenate([best[feats + i : feats + i + 1, :] for i in range(feats)], axis=1)
-    span = jnp.concatenate([best[i : i + 1, :] for i in range(feats)], axis=1) - low
-    slope = 2.0 / jnp.maximum(span, 1.0)
-    CB = 64
-
-    @pl.loop(0, cond.shape[0] // CB)
-    def _(i):
-        v = (cond[at(i, CB), :] - low) * slope - 1.0
-        act[at(i, CB), :] = mish_pair(v)[0].astype(bf16)
-
-    def film_on():
-        film_pass(dp_x, 0, (dp, ch)).wait_recv()
-
-        @pl.loop(1, n_hi)
-        def _(i):
-            for l in range(2):
-                film_z(i, l).start()
-
-    ag_z(1, film_on)
-    ag_far(2)
-    ag_x(0)
-
     lens_ref = lens_all.at[at(ch, s)]
 
     def mask(t):
         return wide((lens_ref[...] > t).astype(f32), c)
 
     count = wide(lens_ref[...].astype(f32), c) * GROUP
-    own_x.wait()
-    swap_in_wait(x_raw, 0)
     sb = 256 // frames
     turn = grid_turn(sb, frames)
-    for b in range(s // sb):
-        y = dot_nn(turn, x_raw[pl.ds(b * 256, 256), :])
-        lens_b = lens_ref[pl.ds(b * sb, sb), :]
-        for t in range(frames):
-            keep = wide((lens_b > t).astype(f32), c)
-            xpad[pl.ds((t + 2) * s + b * sb, sb), :] = (y[t * sb : (t + 1) * sb] * keep).astype(bf16)
-
+    sh = 256 // half
+    turn_h = grid_turn(sh, half)
+    hm = half * s
+    back_h = grid_turn(half, sh)
+    dbase = W_DOWN
+    obuf = res.at[pl.ds(0, hm)]
+    taps_in = (bo, be, bo)
+    taps_at = (0, 0, s)
     def conv_fwd(src, base, store):
         @pl.loop(0, c // NB)
         def _(n):
@@ -410,73 +369,119 @@
     def keep_c(part, cols, acc):
         cbuf[part, cols] = acc
 
-    ag_core(0)
-    ag_y(1)
-    ag_own(2)
-    conv_fwd(xpad, W_ONE, keep_c)
-    arrived(small.at[:, pl.ds(0, others)], in_recv.at[2])
-    bias = row(0)
-    arrived(wf_all.at[:, pl.ds(0, 2 * (n_hi - 1) * frp), :], fw_recv.at[1])
-
-    for i in range(2):
-        film_out[i] = dot_nn(act[...], wf_all[i]) + small[pl.ds(6 + i, 1), my_cols]
-    for i in range(1, n_ch):
-        film_swap(i, (ch + i) % n_ch).start()
-    for i in range(2):
-        film[i, :, my_cols] = film_out[i, at(ch, s), :]
-
-    for n in range(c // NB):
-        cols = pl.ds(n * NB, NB)
-        for mi in range(m // MC):
-            res[pl.ds(mi * MC, MC), cols] = dot_nn(xpad[pl.ds(2 * s + mi * MC, MC), :], w_all[W_RES, :, cols])
-    mean, rstd1 = norm_stats(bias)
-    ag_z(2)
-    ag_x(1)
-    for i in range(1, n_ch):
-        swap_in(cot, cot_raw, h2, 1, i).start()
-    arrived(film.at[:, :, pl.ds(0, others)], fo_recv.at[0])
-    for t in range(frames):
-        part = pl.ds(t * s, s)
-        xh = (cbuf[part, :] + bias - mean) * rstd1
-        mi, dmi = mish_pair(xh * row(1) + row(2))
-        xh1[part, :] = xh
-        m1[part, :] = mi
-        dm1[part, :] = dmi
-        hpad[pl.ds((t + 2) * s, s), :] = ((film[0] * mi + film[1]) * mask(t)).astype(bf16)
-    from_y(2, hi)
-    ag_y(2)
-    ag_core(1)
-    conv_fwd(hpad, W_TWO, keep_c)
-    bias = row(3)
-    mean, rstd2 = norm_stats(bias)
-    for t in range(frames):
-        part = pl.ds(t * s, s)
-        xh = (cbuf[part, :] + bias - mean) * rstd2
-        mi, dmi = mish_pair(xh * row(4) + row(5))
-        xh2[part, :] = xh
-        dm2[part, :] = dmi
-        val = ((mi + res[part, :] + row(8)) * mask(t)).astype(bf16)
-        if t % 2 == 0:
-            be[pl.ds(t // 2 * s, s), :] = val
-        else:
-            bo[pl.ds((t // 2 + 1) * s, s), :] = val
-    sh = 256 // half
-    turn_h = grid_turn(sh, half)
-    hm = half * s
-    back_h = grid_turn(half, sh)
-    dbase = W_DOWN
-    obuf = res.at[pl.ds(0, hm)]
-    taps_in = (bo, be, bo)
-    taps_at = (0, 0, s)
-    ag_x(2)
-    own_cot.wait()
-    swap_in_wait(cot_raw, 1)
-    for b in range(s // sh):
-        y = dot_nn(turn_h, cot_raw[pl.ds(b * 256, 256), :])
-        lens_b = lens_ref[pl.ds(b * sh, sh), :]
-        for j in range(half):
-            keep = wide((lens_b > 2 * j).astype(f32), c)
-            gdn[pl.ds(j * s + b * sh, sh), :] = (y[j * sh : (j + 1) * sh] * keep).astype(bf16)
+    stats_of = {}
+
+    def film_on():
+        film_pass(dp_x, 0, (dp, ch)).wait_recv()
+
+        @pl.loop(1, n_hi)
+        def _(i):
+            for l in range(2):
+                film_z(i, l).start()
+
+    def bounds_on():
+        bounds_x().wait_recv()
+        stats[2] = jnp.maximum(stats[0], stats[1])
+        stats[3 + hi] = stats[2]
+        along(lambda h: bounds_z(h).start())
+
+    def small_on():
+        for i in range(1, n_ch):
+            small_swap(i).start()
+
+    def inputs_on():
+        for i in range(1, n_ch):
+            swap_in(inputs, x_raw, m, 0, i).start()
+
+    def cot_on():
+        for i in range(1, n_ch):
+            swap_in(cot, cot_raw, h2, 1, i).start()
+
+    def condition_rows():
+        arrived(stats.at[pl.ds(3, n_hi - 1)], st_recv.at[1])
+        best = stats[3]
+        for h in range(1, n_hi):
+            best = jnp.maximum(best, stats[3 + h])
+        low = -jnp.concatenate([best[feats + i : feats + i + 1, :] for i in range(feats)], axis=1)
+        span = jnp.concatenate([best[i : i + 1, :] for i in range(feats)], axis=1) - low
+        slope = 2.0 / jnp.maximum(span, 1.0)
+        CB = 64
+
+        @pl.loop(0, cond.shape[0] // CB)
+        def _(i):
+            v = (cond[at(i, CB), :] - low) * slope - 1.0
+            act[at(i, CB), :] = mish_pair(v)[0].astype(bf16)
+
+    def film_project():
+        arrived(wf_all.at[:, pl.ds(0, 2 * (n_hi - 1) * frp), :], fw_recv.at[1])
+
+        for i in range(2):
+            film_out[i] = dot_nn(act[...], wf_all[i]) + small[pl.ds(6 + i, 1), my_cols]
+        for i in range(1, n_ch):
+            film_swap(i, (ch + i) % n_ch).start()
+        for i in range(2):
+            film[i, :, my_cols] = film_out[i, at(ch, s), :]
+
+    def input_frames():
+        own_x.wait()
+        swap_in_wait(x_raw, 0)
+        for b in range(s // sb):
+            y = dot_nn(turn, x_raw[pl.ds(b * 256, 256), :])
+            lens_b = lens_ref[pl.ds(b * sb, sb), :]
+            for t in range(frames):
+                keep = wide((lens_b > t).astype(f32), c)
+                xpad[pl.ds((t + 2) * s + b * sb, sb), :] = (y[t * sb : (t + 1) * sb] * keep).astype(bf16)
+
+    def residual():
+        for n in range(c // NB):
+            cols = pl.ds(n * NB, NB)
+            for mi in range(m // MC):
+                res[pl.ds(mi * MC, MC), cols] = dot_nn(xpad[pl.ds(2 * s + mi * MC, MC), :], w_all[W_RES, :, cols])
+
+    def stats_one():
+        arrived(small.at[:, pl.ds(0, others)], in_recv.at[2])
+        stats_of[1] = norm_stats(row(0))
+
+    def stats_two():
+        stats_of[2] = norm_stats(row(3))
+
+    def section_one():
+        arrived(film.at[:, :, pl.ds(0, others)], fo_recv.at[0])
+        mean, rstd1 = stats_of[1]
+        bias = row(0)
+        for t in range(frames):
+            part = pl.ds(t * s, s)
+            xh = (cbuf[part, :] + bias - mean) * rstd1
+            mi, dmi = mish_pair(xh * row(1) + row(2))
+            xh1[part, :] = xh
+            m1[part, :] = mi
+            dm1[part, :] = dmi
+            hpad[pl.ds((t + 2) * s, s), :] = ((film[0] * mi + film[1]) * mask(t)).astype(bf16)
+
+    def section_two():
+        mean, rstd2 = stats_of[2]
+        bias = row(3)
+        for t in range(frames):
+            part = pl.ds(t * s, s)
+            xh = (cbuf[part, :] + bias - mean) * rstd2
+            mi, dmi = mish_pair(xh * row(4) + row(5))
+            xh2[part, :] = xh
+            dm2[part, :] = dmi
+            val = ((mi + res[part, :] + row(8)) * mask(t)).astype(bf16)
+            if t % 2 == 0:
+                be[pl.ds(t // 2 * s, s), :] = val
+            else:
+                bo[pl.ds((t // 2 + 1) * s, s), :] = val
+
+    def cot_frames():
+        own_cot.wait()
+        swap_in_wait(cot_raw, 1)
+        for b in range(s // sh):
+            y = dot_nn(turn_h, cot_raw[pl.ds(b * 256, 256), :])
+            lens_b = lens_ref[pl.ds(b * sh, sh), :]
+            for j in range(half):
+                keep = wide((lens_b > 2 * j).astype(f32), c)
+                gdn[pl.ds(j * s + b * sh, sh), :] = (y[j * sh : (j + 1) * sh] * keep).astype(bf16)
 
     results = []
 
@@ -706,10 +711,10 @@
         gs[8] = jnp.sum(tot, axis=0, keepdims=True)
 
     def norm_back_two():
-        gs[3:6] = norm_back(xh2, dm2, row(4), rstd2, gc2, None)
+        gs[3:6] = norm_back(xh2, dm2, row(4), stats_of[2][1], gc2, None)
 
     def norm_back_one():
-        gs[0:3] = norm_back(xh1, dm1, row(1), rstd1, gc1, film[0])
+        gs[0:3] = norm_back(xh1, dm1, row(1), stats_of[1][1], gc1, film[0])
 
     def film_rows():
         tot1 = jnp.zeros((s, c), f32)
@@ -807,13 +812,23 @@
         conv_grad(src, g, first, t0 - first, t0 - first + nt)
 
     steps = dict(
+        bx=lambda: bounds_x().start(), fx0=lambda: film_x().start(), smallin=small_on, bz=bounds_on, filmon=film_on,
+        inp=inputs_on, cot=cot_on, cond=condition_rows, fdotf=film_project, perm=input_frames, resd=residual,
+        conv1=lambda: conv_fwd(xpad, W_ONE, keep_c), conv2=lambda: conv_fwd(hpad, W_TWO, keep_c),
+        st1=stats_one, st2=stats_two, app1=section_one, app2=section_two, gdnp=cot_frames,
         C2=lambda: ag_core(2), downf=result_rows, gW_DOWN=gw_down, gW_RES=gw_res, gblock=into_block, gres=into_res,
         nb2=norm_back_two, nb1=norm_back_one, filmg=film_rows, fdot=film_start, fz=film_hi, fe=film_end,
         small=small_start, smy=small_to_y, smx=small_to_x, smz=small_to_z, sme=small_end,
         cb2=lambda: conv_bwd(gc2, W_TWO, keep_c), cb1=lambda: conv_bwd(gc1, W_ONE, keep_ig), ig=input_rows,
     )
+    for p in range(3):
+        steps.update({f"far{p}": partial(ag_far, p), f"own{p}": partial(ag_own, p), f"core{p}": partial(ag_core, p)})
+        steps.update({f"xa{p}": partial(from_x, p, yy), f"xb{p}": partial(from_x, p, 1 - yy), f"fy{p}_0": partial(from_y, p, hi)})
+        for j in range(1, 4):
+            steps[f"fz{p}_{j}"] = partial(from_one, from_z, "z", p, j)
+            steps[f"fy{p}_{j}"] = partial(from_one, from_y, "y", p, j)
     sums = dict(s=rs_start, c=rs_after_core, x=rs_after_x, y=rs_after_y, z=rs_after_z)
-    for name in BACKWARD:
+    for name in ORDER:
         kind, _, group = name.partition("_")
         if name in steps:
             steps[name]()

time: 117 us -> 113 us (0.966)
  Pallas kernels: 116 us -> 112 us
    pallas_call x1, Pallas kernels: 112 us -> 108 us  [block_step(): pl.pallas_call(partial(step_kernel, n_dp, n_ch), out_shape=out, in_specs=...]
where the time goes in v4:
time: 113 us
  Pallas kernels  112 us (99%)
    pallas_call x1, Pallas kernels, block_step(): pl.pallas_call(partial(step_kernel, n_dp, n_ch), out_shape=out, in_specs=...  108 us
    pallas_call x1, Pallas kernels, update(): pl.pallas_call(partial(update_kernel, n), out_shape=[jax.ShapeDtypeStruct...  4.25 us

profile of v4, /device:TPU:0, one launch (start us, length us, event | category | flops | bytes accessed | tf_op | source)
XLA Modules:
  0.0 113.3 jit_solution(11399190521930310383)
XLA Ops:
  0.7 108.2 %block_step.1 = (bf16[2048,128]{1,0:T(8,128)(2,1)}, bf16[4096,128]{1,0:T(8,128)(2,1)}, f32[14,64,128]{2,1,0:T(8,128)}, f32[2,144,128]{2,1,0:T(8,128)}, f32[16,128]{1,0:T(8,128)}) custom-call(bf16[4096,128]{1,0:T(8,128)(2,1)} %inputs.1, bf16[2048,128]{1,0:T(8,128)(2,1)} %cot.1, f32[256,1152]{1,0:T(8,128)} %cond_h.1, s32[1,256]{1,0:T(1,128)} %bitcast.31, ...), custom_call_target="tpu_custom_call" | custom-call | tf_op jit(solution)/shard_map/block_step/pallas_call | solution.py:896
  108.8 4.3 %update.1 = (bf16[2048,128]{1,0:T(8,128)(2,1)}, bf16[4096,128]{1,0:T(8,128)(2,1)}, f32[5,64,128]{2,1,0:T(8,128)}, f32[5,64,128]{2,1,0:T(8,128)}, f32[5,64,128]{2...) custom-call(bf16[2048,128]{1,0:T(8,128)(2,1)} %get-tuple-element.45., ...), custom_call_target="tpu_custom_call" | custom-call | tf_op jit(solution)/shard_map/update/pallas_call | solution.py:983
